TPU v7x, 32 devices: a whole 2x2x4 slice. The times are simulated.
32 devices in a mesh: dp: 2 (over x), ctx: 4 (over y, core), tp: 4 (over z).
Axes of the slice: x: 2, y: 2, z: 4, core: 2. Of those that a mesh axis runs over, the one named last changes fastest.
Arguments:
- block_input: bfloat16 [2, 8, 256, 2048], P('dp', 'ctx', 'tp'), may hold values from -6 to 6
- block_order: int32 [2, 8], P('dp'), may hold values from 0 to 7, each once within a row
- w_qkv: bfloat16 [2048, 3, 2048], P(('dp', 'ctx'), None, 'tp'), may hold values from -1 to 1
- w_out: bfloat16 [2048, 2048], P('tp', ('dp', 'ctx')), may hold values from -3 to 3
- gain_attn: bfloat16 [2048], P(('dp', 'ctx')), may hold values from 0.5 to 1.5
- w_gate_up: bfloat16 [2048, 2, 8192], P(('dp', 'ctx'), None, 'tp'), may hold values from -0.125 to 0.125
- w_down: bfloat16 [8192, 2048], P('tp', ('dp', 'ctx')), may hold values from -0.0625 to 0.0625
- gain_mlp: bfloat16 [2048], P(('dp', 'ctx')), may hold values from 0.5 to 1.5
- cotangent: bfloat16 [2, 8, 256, 2048], P('dp', 'ctx', 'tp'), may hold values from -6 to 6
Outputs:
- block_output: bfloat16 [2, 8, 256, 2048], P('dp', 'ctx', 'tp')
- input_grad: float32 [2, 8, 256, 2048], P('dp', 'ctx', 'tp')
- grad_qkv: float32 [2048, 3, 2048], P(('dp', 'ctx'), None, 'tp')
- grad_out: float32 [2048, 2048], P('tp', ('dp', 'ctx'))
- grad_gain_attn: float32 [2048], P(('dp', 'ctx'))
- grad_gate_up: float32 [2048, 2, 8192], P(('dp', 'ctx'), None, 'tp')
- grad_down: float32 [8192, 2048], P('tp', ('dp', 'ctx'))
- grad_gain_mlp: float32 [2048], P(('dp', 'ctx'))
Inputs may be any that keep to these rules, and one draw needn't show every extreme that they name: `block_order`: each row lists every block number of one sequence once.
All inputs are finite; a program needn't handle non-finite values.
Results may differ from a plain program's by a relative error of at most 0.019.
Values may be sent and summed in bfloat16 or wider, within the bound.
A program may use at most 192 MiB of HBM per device.

v0:
```python
import jax
import jax.numpy as jnp
from jax import lax
from jax.sharding import PartitionSpec as P

HEAD_DIM = 64


EPSILON = 1e-05
ROPE_BASE = 130000.0
NEG_LARGE = -1e30


def rope_tables(positions, head_size):
    half = head_size // 2
    freq = ROPE_BASE ** (-(jnp.arange(half, dtype=jnp.float32) * 2.0 / head_size))
    angle = positions.astype(jnp.float32)[..., None] * freq
    cosine = jnp.cos(angle)
    sine = jnp.sin(angle)
    return (jnp.concatenate([cosine, cosine], -1), jnp.concatenate([sine, sine], -1))


def rotate(values):
    half = values.shape[-1] // 2
    return jnp.concatenate([-values[..., half:], values[..., :half]], -1)


def unrotate(values):
    half = values.shape[-1] // 2
    return jnp.concatenate([values[..., half:], -values[..., :half]], -1)


def rope_apply(values, cosine, sine):
    return values * cosine + rotate(values) * sine


def rope_back(grads, cosine, sine):
    return grads * cosine + unrotate(grads * sine)


def gather_rows(values):
    return lax.all_gather(values, "tp", axis=2, tiled=True)


def sum_rows(values):
    return lax.psum_scatter(values, "tp", scatter_dimension=2, tiled=True)


def gather_cotangent(values):
    return lax.all_gather(values, "tp", axis=2, tiled=True)


def sum_normed(values):
    return lax.psum_scatter(values, "tp", scatter_dimension=2, tiled=True)


def block_scores(query, key_blk, query_pos, key_pos, head_count):
    key_heads = key_blk.reshape(key_blk.shape[0], head_count, HEAD_DIM)
    scores = jnp.einsum("qhe,khe->hqk", query, key_heads, preferred_element_type=jnp.float32)
    visible = key_pos[None, :] <= query_pos[:, None]
    return jnp.where(visible[None], scores, -jnp.inf)


def online_update(state, query, query_pos, key_blk, value_blk, key_pos, head_count):
    run_max, run_sum, run_acc = state
    scores = block_scores(query, key_blk, query_pos, key_pos, head_count)
    new_max = jnp.maximum(run_max, jnp.max(scores, -1))
    factor = jnp.exp(run_max - new_max)
    probs = jnp.exp(scores - new_max[..., None])
    new_sum = run_sum * factor + jnp.sum(probs, -1)
    value_heads = value_blk.reshape(value_blk.shape[0], head_count, HEAD_DIM).astype(jnp.float32)
    mixed = jnp.einsum("hqk,khe->qhe", probs, value_heads, precision=lax.Precision.HIGHEST)
    new_acc = run_acc * factor.T[:, :, None] + mixed
    return (new_max, new_sum, new_acc)


def backward_block(
    query, query_pos, grad_blk, log_total, delta, key_blk, value_blk, key_pos, head_count
):
    scores = block_scores(query, key_blk, query_pos, key_pos, head_count)
    probs = jnp.exp(scores - log_total[..., None])
    value_heads = value_blk.reshape(value_blk.shape[0], head_count, HEAD_DIM)
    key_heads = key_blk.reshape(key_blk.shape[0], head_count, HEAD_DIM)
    dprobs = jnp.einsum("qhe,khe->hqk", grad_blk, value_heads, preferred_element_type=jnp.float32)
    grad_scores = (probs * (dprobs - delta[..., None])).astype(jnp.bfloat16)
    grad_query = jnp.einsum(
        "hqk,khe->qhe", grad_scores, key_heads, preferred_element_type=jnp.float32
    )
    grad_key = jnp.einsum("hqk,qhe->khe", grad_scores, query, preferred_element_type=jnp.float32)
    grad_value = jnp.einsum(
        "hqk,qhe->khe", probs.astype(jnp.bfloat16), grad_blk, preferred_element_type=jnp.float32
    )
    flat_width = head_count * HEAD_DIM
    return (grad_query, grad_key.reshape(-1, flat_width), grad_value.reshape(-1, flat_width))


def body(block_input, block_order, w_qkv, w_out, gain_attn, w_gate_up, w_down, gain_mlp, cotangent):
    f32 = jnp.float32
    bf16 = jnp.bfloat16
    seq_count = block_input.shape[0]
    row_count = block_input.shape[2]
    span = row_count * lax.axis_size("tp")
    local_width = w_qkv.shape[2]
    head_count = local_width // HEAD_DIM
    query_rows = 2 * span
    block_total = block_order.shape[1]
    ctx_index = lax.axis_index("ctx")
    my_ids = lax.dynamic_slice_in_dim(block_order, ctx_index * 2, 2, 1)
    offsets = jnp.arange(span, dtype=jnp.int32)
    query_pos = (my_ids[:, :, None] * span + offsets).reshape(seq_count, query_rows)
    cosine, sine = rope_tables(query_pos, HEAD_DIM)
    cosine = cosine[:, :, None, :]
    sine = sine[:, :, None, :]
    full_qkv, full_out, full_gain_attn = (
        lax.all_gather(w_qkv, ("dp", "ctx"), axis=0, tiled=True),
        lax.all_gather(w_out, ("dp", "ctx"), axis=1, tiled=True),
        lax.all_gather(gain_attn, ("dp", "ctx"), axis=0, tiled=True),
    )
    x_float = block_input.astype(f32)
    rms_attn = lax.rsqrt(jnp.mean(x_float * x_float, -1, keepdims=True) + EPSILON)
    unit_attn = x_float * rms_attn
    normed_attn = (unit_attn * full_gain_attn.astype(f32)).astype(bf16)
    normed_attn_full = gather_rows(normed_attn)
    qkv = jnp.einsum("spcd,dte->spcte", normed_attn_full, full_qkv, preferred_element_type=f32)
    qkv = qkv.reshape(seq_count, query_rows, 3, head_count, HEAD_DIM)
    queries = (rope_apply(qkv[:, :, 0], cosine, sine) * 0.125).astype(bf16)
    keys = rope_apply(qkv[:, :, 1], cosine, sine).astype(bf16)
    values = qkv[:, :, 2].astype(bf16)
    key_send = keys.reshape(seq_count, 2, span, local_width)
    value_send = values.reshape(seq_count, 2, span, local_width)
    initial = (
        jnp.full((seq_count, head_count, query_rows), NEG_LARGE, f32),
        jnp.zeros((seq_count, head_count, query_rows), f32),
        jnp.zeros((seq_count, query_rows, head_count, HEAD_DIM), f32),
    )
    key_piece = lax.all_gather(key_send, "ctx", axis=1, tiled=True)
    value_piece = lax.all_gather(value_send, "ctx", axis=1, tiled=True)

    def visit(step_index, inner):
        run_max, run_sum, run_acc = inner
        key_ids = lax.dynamic_index_in_dim(block_order, step_index, 1, False)
        key_blk = lax.dynamic_index_in_dim(key_piece, step_index, 1, False)
        value_blk = lax.dynamic_index_in_dim(value_piece, step_index, 1, False)
        member = 0
        key_pos = key_ids[member] * span + offsets
        operands = (run_max[member], run_sum[member], run_acc[member])

        def update(current, member=member, key_pos=key_pos):
            return online_update(
                current,
                queries[member],
                query_pos[member],
                key_blk[member],
                value_blk[member],
                key_pos,
                head_count,
            )

        result = update(operands)
        maxes = [result[0]]
        sums = [result[1]]
        accs = [result[2]]
        return (jnp.stack(maxes), jnp.stack(sums), jnp.stack(accs))

    run_max, run_sum, run_acc = lax.fori_loop(0, key_piece.shape[1], visit, initial)
    attention = (run_acc / jnp.transpose(run_sum, (0, 2, 1))[..., None]).astype(bf16)
    log_total = run_max + jnp.log(run_sum)
    attn_flat = attention.reshape(seq_count, 2, span, local_width)
    attn_part = jnp.einsum("spce,ed->spcd", attn_flat, full_out, preferred_element_type=f32)
    resid_mid = x_float + sum_rows(attn_part)
    full_gate_up, full_down, full_gain_mlp = (
        lax.all_gather(w_gate_up, ("dp", "ctx"), axis=0, tiled=True),
        lax.all_gather(w_down, ("dp", "ctx"), axis=1, tiled=True),
        lax.all_gather(gain_mlp, ("dp", "ctx"), axis=0, tiled=True),
    )
    rms_mlp = lax.rsqrt(jnp.mean(resid_mid * resid_mid, -1, keepdims=True) + EPSILON)
    unit_mlp = resid_mid * rms_mlp
    normed_mlp = (unit_mlp * full_gain_mlp.astype(f32)).astype(bf16)
    normed_mlp_full = gather_rows(normed_mlp)
    gate_up = jnp.einsum(
        "spcd,dtf->spctf", normed_mlp_full, full_gate_up, preferred_element_type=f32
    )
    gate = gate_up[:, :, :, 0]
    upper = gate_up[:, :, :, 1]
    sigma = jax.nn.sigmoid(gate)
    hidden = (gate * sigma * upper).astype(bf16)
    down_part = jnp.einsum("spcf,fd->spcd", hidden, full_down, preferred_element_type=f32)
    resid_out = resid_mid + sum_rows(down_part)
    block_output = resid_out.astype(bf16)
    back_gate_up, back_down, back_gain_mlp = (full_gate_up, full_down, full_gain_mlp)
    back_qkv, back_out, back_gain_attn = (full_qkv, full_out, full_gain_attn)
    cotan_full = gather_cotangent(cotangent)
    grad_down_local = jnp.einsum("spcf,spcd->fd", hidden, cotan_full, preferred_element_type=f32)
    grad_hidden = jnp.einsum("spcd,fd->spcf", cotan_full, back_down, preferred_element_type=f32)
    act_grad = jnp.stack(
        [grad_hidden * upper * sigma * (1.0 + gate * (1.0 - sigma)), grad_hidden * gate * sigma],
        axis=3,
    ).astype(bf16)
    grad_gate_up_local = jnp.einsum(
        "spcd,spctf->dtf", normed_mlp_full, act_grad, preferred_element_type=f32
    )
    grad_normed_mlp = sum_normed(
        jnp.einsum("spctf,dtf->spcd", act_grad, back_gate_up, preferred_element_type=f32)
    )
    gain_term_mlp = jnp.sum(grad_normed_mlp * unit_mlp, axis=(0, 1, 2))
    scaled_two = grad_normed_mlp * back_gain_mlp.astype(f32)
    grad_mid = cotangent.astype(f32) + rms_mlp * (
        scaled_two - unit_mlp * jnp.mean(scaled_two * unit_mlp, -1, keepdims=True)
    )
    mlp_shares = (
        lax.psum_scatter(
            grad_gate_up_local.astype(jnp.bfloat16), ("dp", "ctx"), scatter_dimension=0, tiled=True
        ).astype(jnp.float32),
        lax.psum_scatter(
            grad_down_local.astype(jnp.bfloat16), ("dp", "ctx"), scatter_dimension=1, tiled=True
        ).astype(jnp.float32),
        lax.psum_scatter(
            gain_term_mlp.astype(jnp.bfloat16), ("dp", "ctx"), scatter_dimension=0, tiled=True
        ).astype(jnp.float32),
    )
    grad_mid_b = grad_mid.astype(bf16)
    mid_full = gather_cotangent(grad_mid_b)
    grad_out_local = jnp.einsum("spce,spcd->ed", attn_flat, mid_full, preferred_element_type=f32)
    grad_attention = jnp.einsum(
        "spcd,ed->spce", mid_full, back_out, preferred_element_type=f32
    ).astype(bf16)
    grad_attention = grad_attention.reshape(seq_count, query_rows, head_count, HEAD_DIM)
    delta = jnp.transpose(
        jnp.sum(grad_attention.astype(f32) * attention.astype(f32), -1), (0, 2, 1)
    )
    all_keys, all_values = (
        lax.all_gather(key_send, "ctx", axis=1, tiled=True),
        lax.all_gather(value_send, "ctx", axis=1, tiled=True),
    )

    def back_step(grad_queries, slot):
        key_ids = lax.dynamic_index_in_dim(block_order, slot, 1, False)
        key_blk = lax.dynamic_index_in_dim(all_keys, slot, 1, False)
        value_blk = lax.dynamic_index_in_dim(all_values, slot, 1, False)
        member = 0
        key_pos = key_ids[member] * span + offsets

        def work(current, member=member, key_pos=key_pos):
            grad_query, grad_key, grad_value = backward_block(
                queries[member],
                query_pos[member],
                grad_attention[member],
                log_total[member],
                delta[member],
                key_blk[member],
                value_blk[member],
                key_pos,
                head_count,
            )
            return (current + grad_query, grad_key, grad_value)

        result = work(grad_queries[member])
        query_list = [result[0]]
        key_list = [result[1]]
        value_list = [result[2]]
        return (jnp.stack(query_list), (jnp.stack(key_list), jnp.stack(value_list)))

    start_grads = jnp.zeros((seq_count, query_rows, head_count, HEAD_DIM), f32)
    grad_queries, (key_terms, value_terms) = lax.scan(
        back_step, start_grads, jnp.arange(block_total, dtype=jnp.int32)
    )
    grad_keys, grad_values = (
        lax.psum_scatter(
            key_terms.astype(jnp.bfloat16), "ctx", scatter_dimension=0, tiled=True
        ).astype(jnp.float32),
        lax.psum_scatter(
            value_terms.astype(jnp.bfloat16), "ctx", scatter_dimension=0, tiled=True
        ).astype(jnp.float32),
    )
    grad_keys = jnp.transpose(grad_keys, (1, 0, 2, 3)).reshape(
        seq_count, query_rows, head_count, HEAD_DIM
    )
    grad_values = jnp.transpose(grad_values, (1, 0, 2, 3)).reshape(
        seq_count, query_rows, head_count, HEAD_DIM
    )
    qkv_grad = jnp.stack(
        [
            rope_back(grad_queries, cosine, sine) * 0.125,
            rope_back(grad_keys, cosine, sine),
            grad_values,
        ],
        axis=2,
    ).astype(bf16)
    qkv_grad = qkv_grad.reshape(seq_count, 2, span, 3, local_width)
    grad_qkv_local = jnp.einsum(
        "spcd,spcte->dte", normed_attn_full, qkv_grad, preferred_element_type=f32
    )
    grad_normed_attn = sum_normed(
        jnp.einsum("spcte,dte->spcd", qkv_grad, back_qkv, preferred_element_type=f32)
    )
    gain_term_attn = jnp.sum(grad_normed_attn * unit_attn, axis=(0, 1, 2))
    scaled_one = grad_normed_attn * back_gain_attn.astype(f32)
    input_grad = grad_mid + rms_attn * (
        scaled_one - unit_attn * jnp.mean(scaled_one * unit_attn, -1, keepdims=True)
    )
    shard_qkv, shard_out, shard_gain_attn = (
        lax.psum_scatter(
            grad_qkv_local.astype(jnp.bfloat16), ("dp", "ctx"), scatter_dimension=0, tiled=True
        ).astype(jnp.float32),
        lax.psum_scatter(
            grad_out_local.astype(jnp.bfloat16), ("dp", "ctx"), scatter_dimension=1, tiled=True
        ).astype(jnp.float32),
        lax.psum_scatter(
            gain_term_attn.astype(jnp.bfloat16), ("dp", "ctx"), scatter_dimension=0, tiled=True
        ).astype(jnp.float32),
    )
    shard_gate_up, shard_down, shard_gain_mlp = mlp_shares
    total_gain_attn, total_gain_mlp = lax.psum((shard_gain_attn, shard_gain_mlp), "tp")
    return (
        block_output,
        input_grad,
        shard_qkv,
        shard_out,
        total_gain_attn,
        shard_gate_up,
        shard_down,
        total_gain_mlp,
    )


def solution(mesh):
    in_specs = (
        P("dp", "ctx", "tp", None),
        P("dp", None),
        P(("dp", "ctx"), None, "tp"),
        P("tp", ("dp", "ctx")),
        P(("dp", "ctx")),
        P(("dp", "ctx"), None, "tp"),
        P("tp", ("dp", "ctx")),
        P(("dp", "ctx")),
        P("dp", "ctx", "tp", None),
    )
    out_specs = (
        P("dp", "ctx", "tp", None),
        P("dp", "ctx", "tp", None),
        P(("dp", "ctx"), None, "tp"),
        P("tp", ("dp", "ctx")),
        P(("dp", "ctx")),
        P(("dp", "ctx"), None, "tp"),
        P("tp", ("dp", "ctx")),
        P(("dp", "ctx")),
    )
    return jax.shard_map(body, mesh=mesh, in_specs=in_specs, out_specs=out_specs, check_vma=False)
```

profile of v0, /device:TPU:0, one launch (start us, length us, event | category | flops | bytes accessed | tf_op | source)
XLA Modules:
  0.0 1424.0 jit_solution(8658560242486038990)
XLA Ops:
  27.8 30.2 %all-gather.15.cloned.1.call-done = bf16[2048,3,512]{2,0,1:T(8,128)(2,1)} async-done(((bf16[256,3,512]{2,0,1:T(8,128)(2,1)}), bf16[2048,3,512]{2,0,1:T(8,128)(2,1)}) %all-gather.15.cloned.1.call-update) | async-done | bytes 6291472 | tf_op jit(solution)/shard_map/all_gather | solution.py:115
  66.9 39.0 %all-gather.13.cloned.1.call-done = bf16[1,2,256,2048]{3,2,1,0:T(8,128)(2,1)} async-done(((bf16[1,2,64,2048]{3,2,1,0:T(8,128)(2,1)}), bf16[1,2,256,2048]{3,2,1,0:T(8,128)(2,1)}) %all-gather.13.cloned.1.call-update) | async-done | bytes 2097168 | tf_op jit(solution)/shard_map/all_gather | solution.py:42
  133.6 15.4 %all-gather.17.cloned.1.call-done = bf16[1,8,256,512]{3,2,0,1:T(8,128)(2,1)} async-done(((bf16[1,2,256,512]{3,2,0,1:T(8,128)(2,1)}), bf16[1,8,256,512]{3,2,0,1:T(8,128)(2,1)}) %all-gather.17.cloned.1.call-update) | async-done | bytes 2097168 | tf_op jit(solution)/shard_map/all_gather | solution.py:136
  152.9 20.7 %all-gather.19.cloned.1.call-done = bf16[1,8,256,512]{3,2,0,1:T(8,128)(2,1)} async-done(((bf16[1,2,256,512]{3,2,0,1:T(8,128)(2,1)}), bf16[1,8,256,512]{3,2,0,1:T(8,128)(2,1)}) %all-gather.19.cloned.1.call-update) | async-done | bytes 2097168 | tf_op jit(solution)/shard_map/all_gather | solution.py:137
  177.6 92.5 %while.34 = (s32[]{:T(128)}, f32[1,8,512]{2,1,0:T(8,128)S(1)}, f32[1,8,512]{2,1,0:T(8,128)S(1)}, f32[1,512,8,64]{1,3,2,0:T(8,128)S(1)}, s32[1,8]{1,0:T(1,128)S(1...) while((s32[]{:T(128)}, f32[1,8,512]{2,1,0:T(8,128)S(1)}, ...), condition=%wide.region_4.5_spmd.clone, body=%wide.region_1.4_spmd.clone.sunk | while | flops 947548928 | bytes 34334904 | solution.py:165
  285.1 67.6 %reduce-scatter.11.cloned.1.call-done = f32[1,2,64,2048]{3,2,1,0:T(8,128)} async-done(((f32[1,2,256,2048]{3,2,1,0:T(8,128)}), f32[1,2,64,2048]{3,2,1,0:T(8,128)}) %reduce-scatter.11.cloned.1.call-update) | async-done | bytes 1048592 | tf_op jit(solution)/shard_map/reduce_scatter | solution.py:46
  361.0 40.7 %all-gather.23.cloned.1.call-done = bf16[1,2,256,2048]{3,2,1,0:T(8,128)(2,1)} async-done(((bf16[1,2,64,2048]{3,2,1,0:T(8,128)(2,1)}), bf16[1,2,256,2048]{3,2,1,0:T(8,128)(2,1)}) %all-gather.23.cloned.1.call-update) | async-done | bytes 2097168 | tf_op jit(solution)/shard_map/all_gather | solution.py:42
  401.7 91.0 %all-gather.25.cloned.1.call-done = bf16[2048,2,2048]{2,0,1:T(8,128)(2,1)} async-done(((bf16[256,2,2048]{2,0,1:T(8,128)(2,1)}), bf16[2048,2,2048]{2,0,1:T(8,128)(2,1)}) %all-gather.25.cloned.1.call-update) | async-done | bytes 16777232 | tf_op jit(solution)/shard_map/all_gather | solution.py:172
  492.7 15.1 %fusion.48 = f32[1,2,256,2,2048]{4,2,3,1,0:T(8,128)} fusion(bf16[2048,2,2048]{2,0,1:T(8,128)(2,1)} %all-gather.25.cloned.1.call-done, bf16[1,2,256,2048]{3,2,1,0:T(8,128)(2,1)} %all-gather.23.cloned.1.call-done), kind=kOutput, calls=%fused_computation.71 | convolution fusion | flops 8589934592 | bytes 27262976 | tf_op jit(solution)/shard_map/spcd,dtf->spctf/dot_general | solution.py:180
  507.8 32.2 %all-gather.29.cloned.1.call-done = bf16[1,2,256,2048]{3,2,1,0:T(8,128)(2,1)} async-done(((bf16[1,2,64,2048]{3,2,1,0:T(8,128)(2,1)}), bf16[1,2,256,2048]{3,2,1,0:T(8,128)(2,1)}) %all-gather.29.cloned.1.call-update) | async-done | bytes 2097168 | tf_op jit(solution)/shard_map/all_gather | solution.py:50
  540.0 56.4 %all-gather.27.cloned.1.call-done = bf16[2048,2048]{1,0:T(8,128)(2,1)} async-done(((bf16[2048,256]{1,0:T(8,128)(2,1)}), bf16[2048,2048]{1,0:T(8,128)(2,1)}) %all-gather.27.cloned.1.call-update) | async-done | bytes 8388624 | tf_op jit(solution)/shard_map/all_gather | solution.py:173
  609.8 13.8 fusion.54
  623.6 76.9 %reduce-scatter.15.cloned.1.call-done = f32[1,2,64,2048]{3,2,1,0:T(8,128)} async-done(((f32[1,2,256,2048]{3,2,1,0:T(8,128)}), f32[1,2,64,2048]{3,2,1,0:T(8,128)}) %reduce-scatter.15.cloned.1.call-update) | async-done | bytes 1048592 | tf_op jit(solution)/shard_map/reduce_scatter | solution.py:54
  704.7 46.0 %all-gather.31.cloned.1.call-done = bf16[1,2,256,2048]{3,2,1,0:T(8,128)(2,1)} async-done(((bf16[1,2,64,2048]{3,2,1,0:T(8,128)(2,1)}), bf16[1,2,256,2048]{3,2,1,0:T(8,128)(2,1)}) %all-gather.31.cloned.1.call-update) | async-done | bytes 2097168 | tf_op jit(solution)/shard_map/all_gather | solution.py:50
  760.7 122.6 %while.35 = (s32[]{:T(128)}, f32[1,512,8,64]{1,3,2,0:T(8,128)}, bf16[8,1,256,512]{3,2,0,1:T(8,128)(2,1)}, bf16[8,1,256,512]{3,2,0,1:T(8,128)(2,1)}, s32[8]{0:T(1...) while((s32[]{:T(128)}, f32[1,512,8,64]{1,3,2,0:T(8,128)}, ...), condition=%wide.wide.region_12.13_spmd.clone, body=%wide.wide.region_11.12_spmd.clone.sunk | while | flops 679871232 | bytes 27977976 | solution.py:264
  927.3 20.3 %reduce-scatter.19.cloned.1.call-done = bf16[2,1,256,512]{3,2,0,1:T(8,128)(2,1)} async-done(((bf16[8,1,256,512]{3,2,0,1:T(8,128)(2,1)}), bf16[2,1,256,512]{3,2,0,1:T(8,128)(2,1)}) %reduce-scatter.19.cloned.1.call-update) | async-done | bytes 524304 | tf_op jit(solution)/shard_map/reduce_scatter | solution.py:271
  978.7 14.6 %bitcast_convert_fusion = bf16[2048,2,2048]{2,0,1:T(8,128)(2,1)} fusion(bf16[2,256,1,2048]{3,1,0,2:T(8,128)(2,1)} %copy-done.35, bf16[2,256,1,2048]{3,1,0,2:T(8,128)(2,1)} %copy-done.34, bf16[1,2,256,2048]{3,2,1,0:T(8,128)(2,1)S(1)} %copy-done.28), kind=kOutput, calls=%fused_computation.58 | convolution fusion | flops 8606711808 | bytes 23068672 | tf_op jit(solution)/shard_map/spcd,spctf->dtf/dot_general | solution.py:199
  995.2 27.0 %reduce-scatter.29.cloned.1.call-done = bf16[2048,256]{1,0:T(8,128)(2,1)} async-done(((bf16[2048,2048]{1,0:T(8,128)(2,1)}), bf16[2048,256]{1,0:T(8,128)(2,1)}) %reduce-scatter.29.cloned.1.call-update) | async-done | bytes 1048592 | tf_op jit(solution)/shard_map/reduce_scatter | solution.py:214
  1024.9 41.6 %reduce-scatter.25.cloned.1.call-done = bf16[512,256]{1,0:T(8,128)(2,1)} async-done(((bf16[512,2048]{1,0:T(8,128)(2,1)}), bf16[512,256]{1,0:T(8,128)(2,1)}) %reduce-scatter.25.cloned.1.call-update) | async-done | bytes 262160 | tf_op jit(solution)/shard_map/reduce_scatter | solution.py:305
  1068.3 77.8 %reduce-scatter.21.cloned.1.call-done = f32[1,2,64,2048]{3,2,1,0:T(8,128)} async-done(((f32[1,2,256,2048]{3,2,1,0:T(8,128)}), f32[1,2,64,2048]{3,2,1,0:T(8,128)}) %reduce-scatter.21.cloned.1.call-update) | async-done | bytes 1048592 | tf_op jit(solution)/shard_map/reduce_scatter | solution.py:54
  1147.7 13.6 all-reduce.3
  1173.9 51.9 %reduce-scatter.13.cloned.1.call-done = f32[1,2,64,2048]{3,2,1,0:T(8,128)} async-done(((f32[1,2,256,2048]{3,2,1,0:T(8,128)}), f32[1,2,64,2048]{3,2,1,0:T(8,128)}) %reduce-scatter.13.cloned.1.call-update) | async-done | bytes 1048592 | tf_op jit(solution)/shard_map/reduce_scatter | solution.py:46
  1228.9 62.4 %reduce-scatter.23.cloned.1.call-done = bf16[256,3,512]{2,0,1:T(8,128)(2,1)} async-done(((bf16[2048,3,512]{2,0,1:T(8,128)(2,1)}), bf16[256,3,512]{2,0,1:T(8,128)(2,1)}) %reduce-scatter.23.cloned.1.call-update) | async-done | bytes 786448 | tf_op jit(solution)/shard_map/reduce_scatter | solution.py:302
  1293.8 117.1 %reduce-scatter.27.cloned.1.call-done = bf16[256,2,2048]{2,0,1:T(8,128)(2,1)} async-done(((bf16[2048,2,2048]{2,0,1:T(8,128)(2,1)}), bf16[256,2,2048]{2,0,1:T(8,128)(2,1)}) %reduce-scatter.27.cloned.1.call-update) | async-done | bytes 2097168 | tf_op jit(solution)/shard_map/reduce_scatter | solution.py:211
  (435 shorter events, 422.9 us)
Async XLA Ops:
  7.2 50.9 %all-gather.15.cloned.1.call-start = ((), (), s32[]{:S(2)}) async-start(), calls=%async_computation.11 | async-start | bytes 7077888 | tf_op jit(solution)/shard_map/all_gather | solution.py:115
  7.9 98.0 %all-gather.13.cloned.1.call-start = ((), (), s32[]{:S(2)}) async-start(), calls=%async_computation.10 | async-start | bytes 2621440 | tf_op jit(solution)/shard_map/all_gather | solution.py:42
  23.0 126.0 %all-gather.17.cloned.1.call-start = ((), (), s32[]{:S(2)}) async-start(), calls=%async_computation.12 | async-start | bytes 2621440 | tf_op jit(solution)/shard_map/all_gather | solution.py:136
  127.5 46.1 %all-gather.19.cloned.1.call-start = ((), (), s32[]{:S(2)}) async-start(), calls=%async_computation.13 | async-start | bytes 2621440 | tf_op jit(solution)/shard_map/all_gather | solution.py:137
  131.1 139.3 %all-gather.21.cloned.1.call-start = ((), (), s32[]{:S(2)}) async-start(), calls=%async_computation.14 | async-start | bytes 2359296 | tf_op jit(solution)/shard_map/all_gather | solution.py:116
  131.7 221.0 %reduce-scatter.11.cloned.1.call-start = ((), (), s32[]{:S(2)}) async-start(), calls=%async_computation.15 | async-start | bytes 5242880 | tf_op jit(solution)/shard_map/reduce_scatter | solution.py:46
  275.5 126.2 %all-gather.23.cloned.1.call-start = ((), (), s32[]{:S(2)}) async-start(), calls=%async_computation.16 | async-start | bytes 2621440 | tf_op jit(solution)/shard_map/all_gather | solution.py:42
  354.2 347.9 %copy-start.1 = (f32[1,2,64,2048]{3,2,1,0:T(8,128)}, f32[1,2,64,2048]{3,2,1,0:T(8,128)S(1)}, u32[]{:S(2)}) copy-start(f32[1,2,64,2048]{3,2,1,0:T(8,128)S(1)} %get-tuple-element.460) | copy-start | bytes 3145732
  355.4 137.4 %all-gather.25.cloned.1.call-start = ((), (), s32[]{:S(2)}) async-start(), calls=%async_computation.17 | async-start | bytes 18874368 | tf_op jit(solution)/shard_map/all_gather | solution.py:172
  359.2 180.8 %all-gather.29.cloned.1.call-start = ((), (), s32[]{:S(2)}) async-start(), calls=%async_computation.20 | async-start | bytes 2621440 | tf_op jit(solution)/shard_map/all_gather | solution.py:50
  360.0 236.4 %all-gather.27.cloned.1.call-start = ((), (), s32[]{:S(2)}) async-start(), calls=%async_computation.18 | async-start | bytes 9437184 | tf_op jit(solution)/shard_map/all_gather | solution.py:173
  360.6 339.9 %reduce-scatter.15.cloned.1.call-start = ((), (), s32[]{:S(2)}) async-start(), calls=%async_computation.21 | async-start | bytes 5242880 | tf_op jit(solution)/shard_map/reduce_scatter | solution.py:54
  623.6 127.2 %all-gather.31.cloned.1.call-start = ((), (), s32[]{:S(2)}) async-start(), calls=%async_computation.22 | async-start | bytes 2621440 | tf_op jit(solution)/shard_map/all_gather | solution.py:50
  704.5 208.9 %reduce-scatter.17.cloned.1.call-start = ((), (), s32[]{:S(2)}) async-start(), calls=%async_computation.23 | async-start | bytes 2621440 | tf_op jit(solution)/shard_map/reduce_scatter | solution.py:268
  883.3 64.3 %reduce-scatter.19.cloned.1.call-start = ((), (), s32[]{:S(2)}) async-start(), calls=%async_computation.24 | async-start | bytes 2621440 | tf_op jit(solution)/shard_map/reduce_scatter | solution.py:271
  883.9 138.4 %reduce-scatter.29.cloned.1.call-start = ((), (), s32[]{:S(2)}) async-start(), calls=%async_computation.29 | async-start | bytes 9437184 | tf_op jit(solution)/shard_map/reduce_scatter | solution.py:214
  893.3 173.2 %reduce-scatter.25.cloned.1.call-start = ((), (), s32[]{:S(2)}) async-start(), calls=%async_computation.27 | async-start | bytes 2359296 | tf_op jit(solution)/shard_map/reduce_scatter | solution.py:305
  898.5 247.6 %reduce-scatter.21.cloned.1.call-start = ((), (), s32[]{:S(2)}) async-start(), calls=%async_computation.25 | async-start | bytes 5242880 | tf_op jit(solution)/shard_map/reduce_scatter | solution.py:54
  956.2 269.6 %reduce-scatter.13.cloned.1.call-start = ((), (), s32[]{:S(2)}) async-start(), calls=%async_computation.19 | async-start | bytes 5242880 | tf_op jit(solution)/shard_map/reduce_scatter | solution.py:46
  969.0 322.3 %reduce-scatter.23.cloned.1.call-start = ((), (), s32[]{:S(2)}) async-start(), calls=%async_computation.26 | async-start | bytes 7077888 | tf_op jit(solution)/shard_map/reduce_scatter | solution.py:302
  977.1 433.8 %reduce-scatter.27.cloned.1.call-start = ((), (), s32[]{:S(2)}) async-start(), calls=%async_computation.28 | async-start | bytes 18874368 | tf_op jit(solution)/shard_map/reduce_scatter | solution.py:211
  993.4 232.4 %copy-start.2 = (f32[1,2,64,2048]{3,2,1,0:T(8,128)S(1)}, f32[1,2,64,2048]{3,2,1,0:T(8,128)}, u32[]{:S(2)}) copy-start(f32[1,2,64,2048]{3,2,1,0:T(8,128)} %copy-done.1) | copy-start | bytes 3145732
  993.4 232.4 %copy-start.7 = (f32[1,2,64,2048]{3,2,1,0:T(8,128)S(1)}, f32[1,2,64,2048]{3,2,1,0:T(8,128)}, u32[]{:S(2)}) copy-start(f32[1,2,64,2048]{3,2,1,0:T(8,128)} %reduce-scatter.15.cloned.1.call-done) | copy-start | bytes 3145732
  993.4 232.4 %copy-start.9 = (bf16[1,2,64,2048]{3,2,1,0:T(8,128)(2,1)S(1)}, bf16[1,2,64,2048]{3,2,1,0:T(8,128)(2,1)}, u32[]{:S(2)}) copy-start(bf16[1,2,64,2048]{3,2,1,0:T(8,128)(2,1)} %param.21) | copy-start | bytes 1572868
  (39 other events, 1022.6 us)
Sparse Core Ops, SparseCore 0:
  9.9 48.1 all-gather.14
  60.2 45.6 all-gather.12
  127.6 21.3 all-gather.16
  151.0 22.5 all-gather.18
  175.3 28.0 all-gather.20
  275.6 77.0 reduce-scatter.10
  355.5 46.1 all-gather.22
  404.2 88.5 all-gather.24
  494.3 45.6 all-gather.28
  541.7 54.6 all-gather.26
  623.7 76.7 reduce-scatter.14
  704.6 46.1 all-gather.30
  883.4 29.9 reduce-scatter.16
  916.4 31.1 reduce-scatter.18
  950.9 71.2 reduce-scatter.28
  1025.3 41.1 reduce-scatter.24
  1069.2 76.7 reduce-scatter.20
  1148.2 77.5 reduce-scatter.12
  1229.2 62.0 reduce-scatter.22
  1294.7 116.1 reduce-scatter.26
where the time goes:
time: 1430 us; the launch traced here: 1420 us
  waiting for transfers between devices  931 us (65%)
  matrix products  222 us (16%)
  local copies, waits for them, and re-layouts  109 us (8%)
  other arithmetic  85.4 us (6%)
  blocking collectives  45.4 us (3%)
  between operations  16 us (1%)
    reduce_scatter x2, waiting for transfers between devices, sum_normed(): return lax.psum_scatter(values, 'tp', scatter_dimension=2, tiled=True)  155 us
    reduce_scatter x2, waiting for transfers between devices, sum_rows(): return lax.psum_scatter(values, 'tp', scatter_dimension=2, tiled=True)  119 us
    reduce_scatter x1, waiting for transfers between devices, body(): lax.psum_scatter(grad_gate_up_local.astype(jnp.bfloat16), ('dp', 'ctx'),...  117 us
    all_gather x1, waiting for transfers between devices, body(): lax.all_gather(w_gate_up, ('dp', 'ctx'), axis=0, tiled=True)  91 us
    all_gather x2, waiting for transfers between devices, gather_rows(): return lax.all_gather(values, 'tp', axis=2, tiled=True)  79.7 us
    all_gather x2, waiting for transfers between devices, gather_cotangent(): return lax.all_gather(values, 'tp', axis=2, tiled=True)  78.2 us
    reduce_scatter x1, waiting for transfers between devices, body(): lax.psum_scatter(grad_qkv_local.astype(jnp.bfloat16), ('dp', 'ctx'), scat...  62.4 us
    all_gather x1, waiting for transfers between devices, body(): lax.all_gather(w_down, ('dp', 'ctx'), axis=1, tiled=True)  56.4 us
  transfers between devices with their start and end apart: 20, of which 19 were waited for; matrix products, arithmetic and copies ran while one was open for 15% of the time, Pallas kernels for 0%

commit v1 on v0

v1 whole, which is shorter than its diff:
```python
import functools

import jax
import jax.numpy as jnp
from jax import lax
from jax.experimental import pallas as pl
from jax.experimental.pallas import tpu as pltpu
from jax.sharding import PartitionSpec as P

HEAD_DIM = 64
PAIR = 2 * HEAD_DIM
NT = (((1,), (1,)), ((), ()))
NN = (((1,), (0,)), ((), ()))
TN = (((0,), (0,)), ((), ()))


def dot(a, b, dims):
    return lax.dot_general(a, b, dims, preferred_element_type=jnp.float32)


def swap_halves(x):
    lane = lax.broadcasted_iota(jnp.int32, x.shape, 1)
    half = HEAD_DIM // 2
    return jnp.where(
        lane % HEAD_DIM < half, pltpu.roll(x, PAIR - half, 1), pltpu.roll(x, half, 1)
    )


def head_part(x, head):
    lane = lax.broadcasted_iota(jnp.int32, x.shape, 1)
    return jnp.where(lane // HEAD_DIM == head, x, jnp.zeros_like(x))


def visible(shape, base, key_off, key_id, query_id, span):
    keys = lax.broadcasted_iota(jnp.int32, shape, 0)
    queries = lax.broadcasted_iota(jnp.int32, shape, 1)
    return keys - queries <= (query_id - key_id) * span


def attend_kernel(order_ref, mine_ref, q_ref, k_ref, v_ref, o_ref, lse_ref, s_ref):
    blocks, span, _ = k_ref.shape
    rows = q_ref.shape[0]
    parts = rows // span

    def one(index, carry):
        head = index // parts
        part = index % parts
        start = pl.multiple_of(part * span, span)
        query = head_part(q_ref[pl.ds(start, span), :], head)
        top = jnp.full((8, span), -1e30, jnp.float32)
        for blk in range(blocks):
            s = dot(k_ref[blk], query, NT)
            seen = visible((span, span), 0, 0, order_ref[blk], mine_ref[part], span)
            s = jnp.where(seen, s, -jnp.inf)
            s_ref[blk] = s
            top = jnp.maximum(top, jnp.max(s.reshape(span // 8, 8, span), 0))
        top = jnp.max(top, 0, keepdims=True)
        total = jnp.zeros((8, span), jnp.float32)
        acc = jnp.zeros((PAIR, span), jnp.float32)
        for blk in range(blocks):
            p = jnp.exp(s_ref[blk] - top)
            total = total + jnp.sum(p.reshape(span // 8, 8, span), 0)
            acc = acc + dot(v_ref[blk], p.astype(jnp.bfloat16), TN)
        total = jnp.sum(total, 0, keepdims=True)
        out = (acc / total).T
        lane = lax.broadcasted_iota(jnp.int32, out.shape, 1)
        old = o_ref[pl.ds(start, span), :]
        o_ref[pl.ds(start, span), :] = jnp.where(
            lane // HEAD_DIM == head, out.astype(o_ref.dtype), old
        )
        lse_ref[0, pl.ds(head * parts + part, 1), :] = top + jnp.log(total)
        return carry

    lax.fori_loop(0, 2 * parts, one, 0)


def attend(order, mine, q, k, v):
    rows, width = q.shape
    blocks, span, _ = k.shape
    pairs = width // PAIR
    parts = rows // span
    return pl.pallas_call(
        attend_kernel,
        out_shape=(
            jax.ShapeDtypeStruct((rows, width), jnp.bfloat16),
            jax.ShapeDtypeStruct((pairs, 2 * parts, span), jnp.float32),
        ),
        grid_spec=pltpu.PrefetchScalarGridSpec(
            num_scalar_prefetch=2,
            grid=(pairs,),
            in_specs=[
                pl.BlockSpec((rows, PAIR), lambda i, *_: (0, i)),
                pl.BlockSpec((blocks, span, PAIR), lambda i, *_: (0, 0, i)),
                pl.BlockSpec((blocks, span, PAIR), lambda i, *_: (0, 0, i)),
            ],
            out_specs=[
                pl.BlockSpec((rows, PAIR), lambda i, *_: (0, i)),
                pl.BlockSpec((1, 2 * parts, span), lambda i, *_: (i, 0, 0)),
            ],
            scratch_shapes=[pltpu.VMEM((blocks, span, span), jnp.float32)],
        ),
        cost_estimate=pl.CostEstimate(
            flops=4 * rows * blocks * span * width * 4,
            bytes_accessed=4 * blocks * span * width + 4 * rows * width,
            transcendentals=rows * blocks * span * width // HEAD_DIM,
        ),
        name="attend",
    )(order, mine, q, k, v)


def attend_back_kernel(
    order_ref, mine_ref, q_ref, k_ref, v_ref, o_ref, g_ref, lse_ref, cos_ref, sin_ref,
    qcos_ref, qsin_ref, dq_ref, dk_ref, dv_ref, dk_acc, dv_acc, dq_acc, kt_ref, delta_ref,
):
    blocks, span, _ = k_ref.shape
    rows = q_ref.shape[0]
    parts = rows // span
    f32 = jnp.float32
    bf16 = jnp.bfloat16
    for blk in range(blocks):
        kt_ref[blk] = k_ref[blk].T
        dk_acc[blk] = jnp.zeros((span, PAIR), f32)
        dv_acc[blk] = jnp.zeros((span, PAIR), f32)
    for part in range(parts):
        take = pl.ds(part * span, span)
        both = (g_ref[take, :].astype(f32) * o_ref[take, :].astype(f32)).T
        for head in range(2):
            delta_ref[pl.ds(head * parts + part, 1), :] = jnp.sum(
                both[head * HEAD_DIM : (head + 1) * HEAD_DIM], 0, keepdims=True
            )
        dq_acc[part] = jnp.zeros((PAIR, span), f32)

    def one(index, carry):
        head = index // parts
        part = index % parts
        start = pl.multiple_of(part * span, span)
        query = head_part(q_ref[pl.ds(start, span), :], head)
        grad = head_part(g_ref[pl.ds(start, span), :], head)
        lse = lse_ref[0, pl.ds(index, 1), :]
        delta = delta_ref[pl.ds(index, 1), :]
        dq = jnp.zeros((PAIR, span), f32)
        for blk in range(blocks):
            s = dot(k_ref[blk], query, NT)
            seen = visible((span, span), 0, 0, order_ref[blk], mine_ref[part], span)
            p = jnp.exp(jnp.where(seen, s - lse, -jnp.inf))
            dp = dot(v_ref[blk], grad, NT)
            ds = (p * (dp - delta)).astype(bf16)
            dv_acc[blk] += dot(p.astype(bf16), grad, NN)
            dk_acc[blk] += dot(ds, query, NN)
            dq = dq + dot(kt_ref[blk], ds, NN)
        sub = lax.broadcasted_iota(jnp.int32, dq.shape, 0)
        dq_acc[part] += jnp.where(sub // HEAD_DIM == head, dq, 0.0)
        return carry

    lax.fori_loop(0, 2 * parts, one, 0)
    for part in range(parts):
        take = pl.ds(part * span, span)
        dq = dq_acc[part].T
        dq = dq * qcos_ref[take, :] - swap_halves(dq) * qsin_ref[take, :]
        dq_ref[take, :] = (dq * 0.125).astype(bf16)
    for blk in range(blocks):
        dk = dk_acc[blk]
        dk = dk * cos_ref[blk] - swap_halves(dk) * sin_ref[blk]
        dk_ref[blk] = dk.astype(bf16)
        dv_ref[blk] = dv_acc[blk].astype(bf16)


def attend_back(order, mine, q, k, v, o, g, lse, cos, sin, qcos, qsin):
    rows, width = q.shape
    blocks, span, _ = k.shape
    pairs = width // PAIR
    parts = rows // span
    row_spec = pl.BlockSpec((rows, PAIR), lambda i, *_: (0, i))
    blk_spec = pl.BlockSpec((blocks, span, PAIR), lambda i, *_: (0, 0, i))
    tab_spec = pl.BlockSpec((blocks, span, PAIR), lambda i, *_: (0, 0, 0))
    qtab_spec = pl.BlockSpec((rows, PAIR), lambda i, *_: (0, 0))
    f32 = jnp.float32
    return pl.pallas_call(
        attend_back_kernel,
        out_shape=(
            jax.ShapeDtypeStruct((rows, width), jnp.bfloat16),
            jax.ShapeDtypeStruct((blocks, span, width), jnp.bfloat16),
            jax.ShapeDtypeStruct((blocks, span, width), jnp.bfloat16),
        ),
        grid_spec=pltpu.PrefetchScalarGridSpec(
            num_scalar_prefetch=2,
            grid=(pairs,),
            in_specs=[
                row_spec, blk_spec, blk_spec, row_spec, row_spec,
                pl.BlockSpec((1, 2 * parts, span), lambda i, *_: (i, 0, 0)),
                tab_spec, tab_spec, qtab_spec, qtab_spec,
            ],
            out_specs=[row_spec, blk_spec, blk_spec],
            scratch_shapes=[
                pltpu.VMEM((blocks, span, PAIR), f32),
                pltpu.VMEM((blocks, span, PAIR), f32),
                pltpu.VMEM((parts, PAIR, span), f32),
                pltpu.VMEM((blocks, PAIR, span), jnp.bfloat16),
                pltpu.VMEM((2 * parts, span), f32),
            ],
        ),
        cost_estimate=pl.CostEstimate(
            flops=10 * rows * blocks * span * width * 4,
            bytes_accessed=8 * blocks * span * width + 8 * rows * width,
            transcendentals=rows * blocks * span * width // HEAD_DIM,
        ),
        name="attend_back",
    )(order, mine, q, k, v, o, g, lse, cos, sin, qcos, qsin)


def project_kernel(x_ref, w_ref, cos_ref, sin_ref, q_ref, k_ref, v_ref):
    which = pl.program_id(0)
    out = dot(x_ref[...], w_ref[...], NN)

    def turned(scale, ref):
        for lane in range(0, out.shape[1], PAIR):
            piece = out[:, lane : lane + PAIR]
            piece = piece * cos_ref[...] + swap_halves(piece) * sin_ref[...]
            ref[:, lane : lane + PAIR] = (piece * scale).astype(ref.dtype)

    @pl.when(which == 0)
    def _():
        turned(0.125, q_ref)

    @pl.when(which == 1)
    def _():
        turned(1.0, k_ref)

    @pl.when(which == 2)
    def _():
        v_ref[...] = out.astype(v_ref.dtype)


def project(x, w, qcos, qsin):
    rows, depth = x.shape
    width = w.shape[1] // 3
    whole = lambda shape: pl.BlockSpec(shape, lambda t: (0,) * len(shape))
    out = jax.ShapeDtypeStruct((rows, width), jnp.bfloat16)
    return pl.pallas_call(
        project_kernel,
        out_shape=(out, out, out),
        grid=(3,),
        in_specs=[
            whole((rows, depth)),
            pl.BlockSpec((depth, width), lambda t: (0, t)),
            whole((rows, PAIR)),
            whole((rows, PAIR)),
        ],
        out_specs=[whole((rows, width))] * 3,
        cost_estimate=pl.CostEstimate(
            flops=2 * rows * depth * 3 * width,
            bytes_accessed=2 * depth * 3 * width + 2 * rows * depth,
            transcendentals=0,
        ),
        name="project",
    )(x, w, qcos, qsin)


def neighbour_barrier(line_axis, cube_axis):
    sem = pltpu.get_barrier_semaphore()
    count = 0
    if line_axis is not None:
        me = lax.axis_index(line_axis)
        size = lax.axis_size(line_axis)

        @pl.when(me > 0)
        def _():
            pl.semaphore_signal(sem, inc=1, device_id={line_axis: me - 1}, device_id_type=MESH)

        @pl.when(me < size - 1)
        def _():
            pl.semaphore_signal(sem, inc=1, device_id={line_axis: me + 1}, device_id_type=MESH)

    if cube_axis is not None:
        for bit in cube_bits(lax.axis_size(cube_axis)):
            pl.semaphore_signal(
                sem, inc=1, device_id={cube_axis: flipped(lax.axis_index(cube_axis), bit)},
                device_id_type=MESH,
            )
            count += 1
    if line_axis is not None:

        @pl.when((me > 0) & (me < size - 1))
        def _():
            pl.semaphore_wait(sem, count + 2)

        @pl.when((me == 0) | (me == size - 1))
        def _():
            pl.semaphore_wait(sem, count + 1)

    else:
        pl.semaphore_wait(sem, count)


def cube_bits(size):
    bits = []
    while size > 1:
        size //= 2
        bits.append(size)
    return bits


def flipped(index, bit):
    return index + bit - 2 * bit * ((index // bit) % 2)


def flip_all(index, mask):
    bit = 1
    while bit <= mask:
        if mask // bit % 2:
            index = flipped(index, bit)
        bit *= 2
    return index


def remote(src, dst, send, recv, axis, target):
    return pltpu.make_async_remote_copy(
        src_ref=src, dst_ref=dst, send_sem=send, recv_sem=recv,
        device_id={axis: target}, device_id_type=MESH,
    )


def row_gather_steps(axis, x_ref, o_ref, send, recv, local):
    size = lax.axis_size(axis)
    me = lax.axis_index(axis)
    pieces = x_ref.shape[0]
    own = [
        pltpu.make_async_copy(x_ref.at[p], o_ref.at[p, me], local.at[p]) for p in range(pieces)
    ]

    def copy(way, step, p):
        block = me - step if way == 0 else me + step
        src = x_ref.at[p] if step == 0 else o_ref.at[p, block]
        return remote(
            src, o_ref.at[p, block], send.at[way, step, p], recv.at[way, step, p],
            axis, me + 1 if way == 0 else me - 1,
        )

    def sends(way, step):
        if way == 0:
            return (me < size - 1) & (me - step >= 0)
        return (me > 0) & (me + step < size)

    def arrives(way, step):
        return me - 1 - step >= 0 if way == 0 else me + 1 + step < size

    def arrival(way, step, p):
        block = me - 1 - step if way == 0 else me + 1 + step
        return remote(
            o_ref.at[p, block], o_ref.at[p, block], send.at[way, step, p],
            recv.at[way, step, p], axis, me - 1 if way == 0 else me + 1,
        )

    for step in range(size):
        for p in range(pieces):
            for way in (0, 1):
                if step > 0:

                    @pl.when(arrives(way, step - 1))
                    def _(way=way, p=p):
                        arrival(way, step - 1, p).wait_recv()

                if step < size - 1:

                    @pl.when(sends(way, step))
                    def _(way=way, p=p):
                        copy(way, step, p).start()

        if step == 0:
            for one in own:
                one.start()
        yield
    for one in own:
        one.wait()
    for step in range(size - 1):
        for way in (0, 1):

            @pl.when(sends(way, step))
            def _(way=way):
                for p in range(pieces):
                    copy(way, step, p).wait_send()


def row_gather_scratch(size, pieces):
    return [
        pltpu.SemaphoreType.DMA((2, size - 1, pieces)),
        pltpu.SemaphoreType.DMA((2, size - 1, pieces)),
        pltpu.SemaphoreType.DMA((pieces,)),
    ]


def row_scatter_steps(axis, part_ref, o_ref, inbox, outbox, send, recv):
    size = lax.axis_size(axis)
    me = lax.axis_index(axis)
    pieces = part_ref.shape[0]
    f32 = jnp.float32

    def target(way, step):
        return size - 1 - step if way == 0 else step

    def from_edge(way):
        return me == 0 if way == 0 else me == size - 1

    def passes(way, step):
        dest = target(way, step)
        return dest > me if way == 0 else dest < me

    def arrives(way, step):
        dest = target(way, step)
        return (me > 0) & (dest >= me) if way == 0 else (me < size - 1) & (dest <= me)

    def copy(way, step, p, edge):
        src = part_ref.at[p, target(way, step)] if edge else outbox.at[way, step, p]
        return remote(
            src, inbox.at[way, step, p], send.at[way, step, p], recv.at[way, step, p],
            axis, me + 1 if way == 0 else me - 1,
        )

    def arrival(way, step, p):
        return remote(
            inbox.at[way, step, p], inbox.at[way, step, p], send.at[way, step, p],
            recv.at[way, step, p], axis, me - 1 if way == 0 else me + 1,
        )

    for step in range(size - 1):
        for p in range(pieces):
            for way in (0, 1):

                @pl.when(arrives(way, step))
                def _(way=way, p=p):
                    arrival(way, step, p).wait_recv()

                @pl.when(passes(way, step) & from_edge(way))
                def _(way=way, p=p):
                    copy(way, step, p, True).start()

                @pl.when(passes(way, step) & jnp.logical_not(from_edge(way)))
                def _(way=way, p=p):
                    outbox[way, step, p] = (
                        inbox[way, step, p].astype(f32)
                        + part_ref[p, target(way, step)].astype(f32)
                    ).astype(outbox.dtype)
                    copy(way, step, p, False).start()

        yield
    for p in range(pieces):
        own = part_ref[p, me].astype(f32)

        @pl.when(me == 0)
        def _(p=p, own=own):
            o_ref[p] = own + inbox[1, me, p].astype(f32)

        @pl.when(me == size - 1)
        def _(p=p, own=own):
            o_ref[p] = own + inbox[0, size - 1 - me, p].astype(f32)

        @pl.when((me > 0) & (me < size - 1))
        def _(p=p, own=own):
            o_ref[p] = own + (
                inbox[0, size - 1 - me, p].astype(f32) + inbox[1, me, p].astype(f32)
            )

    for step in range(size - 1):
        for way in (0, 1):

            @pl.when(passes(way, step))
            def _(way=way):
                for p in range(pieces):
                    copy(way, step, p, False).wait_send()


def row_scatter_scratch(size, block):
    pieces = block[0]
    return [
        pltpu.VMEM((2, size - 1) + block, jnp.bfloat16),
        pltpu.VMEM((2, size - 1) + block, jnp.bfloat16),
        pltpu.SemaphoreType.DMA((2, size - 1, pieces)),
        pltpu.SemaphoreType.DMA((2, size - 1, pieces)),
    ]


def cube_gather_steps(axis, x_refs, o_refs, send, recv, local):
    size = lax.axis_size(axis)
    me = lax.axis_index(axis)
    bits = cube_bits(size)
    count = len(x_refs)
    own = [
        pltpu.make_async_copy(x_refs[t], o_refs[t].at[me], local.at[t]) for t in range(count)
    ]

    def copy(mask, bit, t):
        block = flip_all(me, mask)
        src = x_refs[t] if mask == 0 else o_refs[t].at[block]
        return remote(
            src, o_refs[t].at[block], send.at[mask + bit, t], recv.at[mask + bit, t],
            axis, flipped(me, bit),
        )

    def arrival(mask, t):
        low = mask & -mask
        block = flip_all(me, mask)
        return remote(
            o_refs[t].at[block], o_refs[t].at[block], send.at[mask, t], recv.at[mask, t],
            axis, flipped(me, low),
        )

    waited = set()
    masks = [0]
    for bit in bits:
        for t in range(count):
            copy(0, bit, t).start()
    for one in own:
        one.start()
    yield
    for level, bit in enumerate(bits):
        for mask in masks:
            if mask == 0:
                continue
            for t in range(count):
                if (mask, t) not in waited:
                    arrival(mask, t).wait_recv()
                    waited.add((mask, t))
                copy(mask, bit, t).start()
        masks = masks + [mask + bit for mask in masks]
        yield
    for mask in masks:
        for t in range(count):
            if mask and (mask, t) not in waited:
                arrival(mask, t).wait_recv()
    for one in own:
        one.wait()
    for mask in masks:
        for t in range(count):
            if mask:
                low = mask & -mask
                copy(mask - low, low, t).wait_send()


def cube_gather_scratch(size, count):
    return [
        pltpu.SemaphoreType.DMA((size, count)),
        pltpu.SemaphoreType.DMA((size, count)),
        pltpu.SemaphoreType.DMA((count,)),
    ]


def cube_scatter_steps(axis, x_refs, o_refs, inbox, total, outbox, send, recv):
    size = lax.axis_size(axis)
    me = lax.axis_index(axis)
    bits = cube_bits(size)[::-1]
    count = len(x_refs)
    f32 = jnp.float32
    kept = list(range(size))[::-1]
    first = True
    for bit in bits:
        going = [mask for mask in kept if mask & bit]
        kept = [mask for mask in kept if not mask & bit]

        def copy(mask, t, bit=bit, first=first):
            src = x_refs[t].at[flip_all(me, mask)] if first else outbox.at[mask, t]
            return remote(
                src, inbox.at[mask, t], send.at[mask, t], recv.at[mask, t],
                axis, flipped(me, bit),
            )

        for mask in going:
            for t in range(count):
                if not first:
                    outbox[mask, t] = total[mask, t].astype(outbox.dtype)
                copy(mask, t).start()
        yield
        for mask in kept:
            for t in range(count):
                copy(mask + bit, t).wait_recv()
                if first:
                    base = x_refs[t][flip_all(me, mask)].astype(f32)
                else:
                    base = total[mask, t]
                total[mask, t] = base + inbox[mask + bit, t].astype(f32)
        for mask in going:
            for t in range(count):
                copy(mask, t).wait_send()
        first = False
    for t in range(count):
        o_refs[t][...] = total[0, t].astype(o_refs[t].dtype)


def cube_scatter_scratch(size, block, count):
    return [
        pltpu.VMEM((size, count) + block, jnp.bfloat16),
        pltpu.VMEM((size, count) + block, jnp.float32),
        pltpu.VMEM((size, count) + block, jnp.bfloat16),
        pltpu.SemaphoreType.DMA((size, count)),
        pltpu.SemaphoreType.DMA((size, count)),
    ]


def run_steps(*walks):
    walks = list(walks)
    while walks:
        for walk in list(walks):
            try:
                next(walk)
            except StopIteration:
                walks.remove(walk)


ANY = pl.BlockSpec(memory_space=pl.ANY)
IN_VMEM = pl.BlockSpec(memory_space=pltpu.VMEM)


def comm_params(number):
    return pltpu.CompilerParams(
        collective_id=number, has_side_effects=True, vmem_limit_bytes=48 * 1024 * 1024
    )


def comm_cost(size):
    return pl.CostEstimate(flops=0, bytes_accessed=size, transcendentals=0)


def gather_rows(x, number):
    pieces, rows, depth = x.shape
    size = lax.axis_size("tp")

    def kernel(x_ref, o_ref, send, recv, local):
        neighbour_barrier("tp", None)
        run_steps(row_gather_steps("tp", x_ref, o_ref, send, recv, local))

    return pl.pallas_call(
        kernel,
        out_shape=jax.ShapeDtypeStruct((pieces, size, rows, depth), x.dtype),
        in_specs=[IN_VMEM],
        out_specs=ANY,
        scratch_shapes=row_gather_scratch(size, pieces),
        compiler_params=comm_params(number),
        cost_estimate=comm_cost(COMM_BYTES),
        name="gather_rows",
    )(x)


def scatter_rows(part, number):
    pieces, size, rows, depth = part.shape

    def kernel(part_ref, o_ref, *scratch):
        neighbour_barrier("tp", None)
        run_steps(row_scatter_steps("tp", part_ref, o_ref, *scratch))

    return pl.pallas_call(
        kernel,
        out_shape=jax.ShapeDtypeStruct((pieces, rows, depth), jnp.float32),
        in_specs=[IN_VMEM],
        out_specs=IN_VMEM,
        scratch_shapes=row_scatter_scratch(size, (pieces, rows, depth)),
        compiler_params=comm_params(number),
        cost_estimate=comm_cost(COMM_BYTES),
        name="scatter_rows",
    )(part)


def gather_blocks(x, keys, values, number):
    pieces, rows, depth = x.shape
    size = lax.axis_size("tp")
    ring = lax.axis_size("ctx")

    def kernel(x_ref, k_ref, v_ref, o_ref, ko_ref, vo_ref, *sems):
        neighbour_barrier("tp", "ctx")
        run_steps(
            cube_gather_steps("ctx", (k_ref, v_ref), (ko_ref, vo_ref), *sems[3:]),
            row_gather_steps("tp", x_ref, o_ref, *sems[:3]),
        )

    blocks = jax.ShapeDtypeStruct((ring,) + keys.shape, keys.dtype)
    return pl.pallas_call(
        kernel,
        out_shape=(jax.ShapeDtypeStruct((pieces, size, rows, depth), x.dtype), blocks, blocks),
        in_specs=[IN_VMEM] * 3,
        out_specs=[ANY] * 3,
        scratch_shapes=row_gather_scratch(size, pieces) + cube_gather_scratch(ring, 2),
        compiler_params=comm_params(number),
        cost_estimate=comm_cost(COMM_BYTES),
        name="gather_blocks",
    )(x, keys, values)


def scatter_blocks(part, dk, dv, number):
    pieces, size, rows, depth = part.shape
    ring = dk.shape[0]

    def kernel(part_ref, k_ref, v_ref, o_ref, ko_ref, vo_ref, *scratch):
        neighbour_barrier("tp", "ctx")
        run_steps(
            cube_scatter_steps("ctx", (k_ref, v_ref), (ko_ref, vo_ref), *scratch[4:]),
            row_scatter_steps("tp", part_ref, o_ref, *scratch[:4]),
        )

    block = jax.ShapeDtypeStruct(dk.shape[1:], jnp.bfloat16)
    return pl.pallas_call(
        kernel,
        out_shape=(jax.ShapeDtypeStruct((pieces, rows, depth), jnp.float32), block, block),
        in_specs=[IN_VMEM] * 3,
        out_specs=[IN_VMEM] * 3,
        scratch_shapes=row_scatter_scratch(size, (pieces, rows, depth))
        + cube_scatter_scratch(ring, dk.shape[1:], 2),
        compiler_params=comm_params(number),
        cost_estimate=comm_cost(COMM_BYTES),
        name="scatter_blocks",
    )(part, dk, dv)


EPSILON = 1e-05
ROPE_BASE = 130000.0
COMM_BYTES = 64 * 1024 * 1024
MESH = pl.DeviceIdType.MESH


def rope_tables(positions):
    half = HEAD_DIM // 2
    lane = jnp.arange(PAIR, dtype=jnp.int32)
    freq = ROPE_BASE ** (-((lane % half).astype(jnp.float32) * 2.0 / HEAD_DIM))
    angle = positions.astype(jnp.float32)[..., None] * freq
    sign = jnp.where(lane % HEAD_DIM < half, -1.0, 1.0)
    return jnp.cos(angle), jnp.sin(angle) * sign


def body(block_input, block_order, w_qkv, w_out, gain_attn, w_gate_up, w_down, gain_mlp, cotangent):
    f32 = jnp.float32
    bf16 = jnp.bfloat16
    shards = ("dp", "ctx")
    _, pieces, row_count, depth = block_input.shape
    span = row_count * lax.axis_size("tp")
    width = w_qkv.shape[2]
    units = w_gate_up.shape[2]
    shard = w_qkv.shape[0]
    rows = pieces * span
    block_total = block_order.shape[1]
    order = block_order[0]
    first = lax.axis_index("ctx") * pieces
    mine = lax.dynamic_slice_in_dim(order, first, pieces, 0)
    offsets = jnp.arange(span, dtype=jnp.int32)
    cos, sin = rope_tables(order[:, None] * span + offsets)
    qcos, qsin = (
        lax.dynamic_slice_in_dim(t, first, pieces, 0).reshape(rows, PAIR) for t in (cos, sin)
    )

    gain_one = gain_attn.astype(f32)[:, None]
    gain_two = gain_mlp.astype(f32)[:, None]
    flat_qkv = w_qkv.reshape(shard, 3 * width).astype(f32)
    flat_gate_up = w_gate_up.reshape(shard, 2 * units).astype(f32)
    full_qkv = lax.all_gather((flat_qkv * gain_one).astype(bf16), shards, axis=0, tiled=True)
    full_out = lax.all_gather(w_out, shards, axis=1, tiled=True)
    full_gate_up = lax.all_gather(
        (flat_gate_up * gain_two).astype(bf16), shards, axis=0, tiled=True
    )
    full_down = lax.all_gather(w_down, shards, axis=1, tiled=True)

    x = block_input[0].astype(f32)
    rms_attn = lax.rsqrt(jnp.mean(x * x, -1, keepdims=True) + EPSILON)
    unit_attn = x * rms_attn
    unit_attn_full = gather_rows(unit_attn.astype(bf16), 0).reshape(rows, depth)
    queries, keys, values = project(unit_attn_full, full_qkv, qcos, qsin)
    cotan_full, key_blocks, value_blocks = gather_blocks(cotangent[0], keys, values, 1)
    cotan_full = cotan_full.reshape(rows, depth)
    key_blocks = key_blocks.reshape(block_total, span, width)
    value_blocks = value_blocks.reshape(block_total, span, width)
    attention, lse = attend(order, mine, queries, key_blocks, value_blocks)

    def spread(part):
        return part.astype(bf16).reshape(pieces, -1, row_count, depth)

    attn_part = jnp.dot(attention, full_out, preferred_element_type=f32)
    resid_mid = x + scatter_rows(spread(attn_part), 2)
    rms_mlp = lax.rsqrt(jnp.mean(resid_mid * resid_mid, -1, keepdims=True) + EPSILON)
    unit_mlp = resid_mid * rms_mlp
    unit_mlp_full = gather_rows(unit_mlp.astype(bf16), 3).reshape(rows, depth)
    gate_up = jnp.dot(unit_mlp_full, full_gate_up, preferred_element_type=f32)
    gate = gate_up[:, :units]
    upper = gate_up[:, units:]
    sigma = jax.nn.sigmoid(gate)
    hidden = (gate * sigma * upper).astype(bf16)
    grad_hidden = lax.dot_general(cotan_full, full_down, NT, preferred_element_type=f32)
    act_grad = jnp.concatenate(
        [grad_hidden * upper * sigma * (1.0 + gate * (1.0 - sigma)), grad_hidden * gate * sigma],
        axis=1,
    ).astype(bf16)
    grad_down_local = lax.dot_general(hidden, cotan_full, TN, preferred_element_type=f32)
    share_down = lax.psum_scatter(
        grad_down_local.astype(bf16), shards, scatter_dimension=1, tiled=True
    )
    grad_gate_up_local = lax.dot_general(unit_mlp_full, act_grad, TN, preferred_element_type=f32)
    share_gate_up = lax.psum_scatter(
        grad_gate_up_local.astype(bf16), shards, scatter_dimension=0, tiled=True
    )
    scaled_part = lax.dot_general(act_grad, full_gate_up, NT, preferred_element_type=f32)
    scaled_two = scatter_rows(spread(scaled_part), 4)
    cotan = cotangent[0].astype(f32)
    grad_mid = cotan + rms_mlp * (
        scaled_two - unit_mlp * jnp.mean(scaled_two * unit_mlp, -1, keepdims=True)
    )
    mid_full = gather_rows(grad_mid.astype(bf16), 5).reshape(rows, depth)
    grad_attention = lax.dot_general(mid_full, full_out, NT, preferred_element_type=f32)
    grad_queries, key_terms, value_terms = attend_back(
        order, mine, queries, key_blocks, value_blocks, attention, grad_attention.astype(bf16),
        lse, cos, sin, qcos, qsin,
    )
    grad_out_local = lax.dot_general(attention, mid_full, TN, preferred_element_type=f32)
    share_out = lax.psum_scatter(
        grad_out_local.astype(bf16), shards, scatter_dimension=1, tiled=True
    )
    down_part = jnp.dot(hidden, full_down, preferred_element_type=f32)
    down_sum, grad_keys, grad_values = scatter_blocks(
        spread(down_part),
        key_terms.reshape(-1, rows, width),
        value_terms.reshape(-1, rows, width),
        6,
    )
    block_output = (resid_mid + down_sum).astype(bf16)
    qkv_grad = jnp.concatenate([grad_queries, grad_keys, grad_values], axis=1)
    grad_qkv_local = lax.dot_general(unit_attn_full, qkv_grad, TN, preferred_element_type=f32)
    share_qkv = lax.psum_scatter(
        grad_qkv_local.astype(bf16), shards, scatter_dimension=0, tiled=True
    )
    scaled_one_part = lax.dot_general(qkv_grad, full_qkv, NT, preferred_element_type=f32)
    scaled_one = scatter_rows(spread(scaled_one_part), 7)
    input_grad = grad_mid + rms_attn * (
        scaled_one - unit_attn * jnp.mean(scaled_one * unit_attn, -1, keepdims=True)
    )
    raw_qkv = share_qkv.astype(f32)
    raw_gate_up = share_gate_up.astype(f32)
    gain_terms = jnp.stack(
        [jnp.sum(raw_qkv * flat_qkv, -1), jnp.sum(raw_gate_up * flat_gate_up, -1)]
    )
    gain_sums = lax.psum(gain_terms, "tp")
    return (
        block_output[None],
        input_grad[None],
        (raw_qkv * gain_one).reshape(shard, 3, width),
        share_out.astype(f32),
        gain_sums[0],
        (raw_gate_up * gain_two).reshape(shard, 2, units),
        share_down.astype(f32),
        gain_sums[1],
    )


def solution(mesh):
    in_specs = (
        P("dp", "ctx", "tp", None),
        P("dp", None),
        P(("dp", "ctx"), None, "tp"),
        P("tp", ("dp", "ctx")),
        P(("dp", "ctx")),
        P(("dp", "ctx"), None, "tp"),
        P("tp", ("dp", "ctx")),
        P(("dp", "ctx")),
        P("dp", "ctx", "tp", None),
    )
    out_specs = (
        P("dp", "ctx", "tp", None),
        P("dp", "ctx", "tp", None),
        P(("dp", "ctx"), None, "tp"),
        P("tp", ("dp", "ctx")),
        P(("dp", "ctx")),
        P(("dp", "ctx"), None, "tp"),
        P("tp", ("dp", "ctx")),
        P(("dp", "ctx")),
    )
    return jax.shard_map(body, mesh=mesh, in_specs=in_specs, out_specs=out_specs, check_vma=False)
```

time: 1430 us -> 935 us (0.65)
  waiting for transfers between devices: 931 us -> 130 us
  Pallas kernels: 0 us -> 611 us
  matrix products: 222 us -> 95.9 us
  local copies, waits for them, and re-layouts: 109 us -> 37.4 us
  other arithmetic: 85.4 us -> 24.3 us
  blocking collectives: 45.4 us -> 11.7 us
    pallas_call x0 -> x11, Pallas kernels: none -> 611 us  [the longest x3 261 us: scatter_rows(): pl.pallas_call(kernel, out_shape=jax.ShapeDtypeStruct((pieces, rows, dept...]
    reduce_scatter x10 -> x4, waiting for transfers between devices: 556 us -> 129 us  [the longest x1 117 us: body(): lax.psum_scatter(grad_gate_up_local.astype(bf16), shards, scatter_dimensi...]
    all_gather x10 -> x4, waiting for transfers between devices: 372 us -> 0.01 us  [the longest x1 0.01 us: body(): lax.all_gather((flat_qkv * gain_one).astype(bf16), shards, axis=0, tiled=...]
    dot_general x68 -> x11, matrix products: 222 us -> 95.9 us  [the longest x1 15.1 us: body(): gate_up = jnp.dot(unit_mlp_full, full_gate_up, preferred_element_type=f32)]
    reduce_sum x12 -> x4, other arithmetic: 29.4 us -> 2.72 us  [the longest x1 1.93 us: body(): jnp.sum(raw_qkv * flat_qkv, -1)]
    dynamic_slice x32 -> x3, local copies, waits for them, and re-layouts: 28.5 us -> 2.06 us  [the longest x2 1.45 us: body(): lax.dynamic_slice_in_dim(t, first, pieces, 0).reshape(rows, PAIR)]
    all_gather x2 -> x0, blocking collectives: 19.3 us -> none  [the longest x1 10.4 us: body(): lax.all_gather(gain_attn, ('dp', 'ctx'), axis=0, tiled=True)]
    unnamed x80 -> x67, local copies, waits for them, and re-layouts: 29.5 us -> 24.6 us
  transfers between devices with their start and end apart: 20 -> 8, of which waited for: 19 -> 2; matrix products, arithmetic and copies ran while one was open for 15% -> 10% of each run, Pallas kernels for 0% -> 50%
where the time goes in v1:
time: 935 us; the launch traced here: 926 us
  Pallas kernels  611 us (65%)
  waiting for transfers between devices  130 us (14%)
  matrix products  95.9 us (10%)
  local copies, waits for them, and re-layouts  37.4 us (4%)
  other arithmetic  24.3 us (3%)
  between operations  14.9 us (2%)
  blocking collectives  11.7 us (1%)
    pallas_call x3, Pallas kernels, scatter_rows(): pl.pallas_call(kernel, out_shape=jax.ShapeDtypeStruct((pieces, rows, dept...  261 us
    pallas_call x3, Pallas kernels, gather_rows(): pl.pallas_call(kernel, out_shape=jax.ShapeDtypeStruct((pieces, size, rows...  139 us
    reduce_scatter x1, waiting for transfers between devices, body(): lax.psum_scatter(grad_gate_up_local.astype(bf16), shards, scatter_dimensi...  117 us
    pallas_call x1, Pallas kernels, scatter_blocks(): pl.pallas_call(kernel, out_shape=(jax.ShapeDtypeStruct((pieces, rows, dep...  94 us
    pallas_call x1, Pallas kernels, gather_blocks(): pl.pallas_call(kernel, out_shape=(jax.ShapeDtypeStruct((pieces, size, row...  41.8 us
    pallas_call x1, Pallas kernels, attend_back(): pl.pallas_call(attend_back_kernel, out_shape=(jax.ShapeDtypeStruct((rows,...  41.3 us
    unnamed x67, local copies, waits for them, and re-layouts  24.6 us
    pallas_call x1, Pallas kernels, attend(): pl.pallas_call(attend_kernel, out_shape=(jax.ShapeDtypeStruct((rows, widt...  24.5 us
  transfers between devices with their start and end apart: 8, of which 2 were waited for; matrix products, arithmetic and copies ran while one was open for 10% of the time, Pallas kernels for 50%

profile of v1, /device:TPU:0, one launch (start us, length us, event | category | flops | bytes accessed | tf_op | source)
XLA Modules:
  0.0 926.1 jit_solution(2450167981157875558)
XLA Ops:
  22.9 39.0 %gather_rows.3 = bf16[2,4,64,2048]{3,2,1,0:T(8,128)(2,1)S(1)} custom-call(bf16[2,64,2048]{2,1,0:T(8,128)(2,1)S(1)} %fusion.4.x_ref), custom_call_target="tpu_custom_call" | custom-call | bytes 67108864 | tf_op jit(solution)/shard_map/gather_rows/pallas_call | solution.py:630
  70.1 8.8 project.1
  81.0 41.8 %gather_blocks.1 = (bf16[2,4,64,2048]{3,2,1,0:T(8,128)(2,1)S(1)}, bf16[4,512,512]{2,1,0:T(8,128)(2,1)S(1)}, bf16[4,512,512]{2,1,0:T(8,128)(2,1)}) custom-call(bf16[2,64,2048]{2,1,0:T(8,128)(2,1)S(1)} %bitcast.75, bf16[512,512]{1,0:T(8,128)(2,1)S(1)} %copy-done.9, bf16[512,512]{1,0:T(8,128)(2,1)S(1)} %copy-done.10), custom_call_target="tpu_custom_call" | custom-call | bytes 67108864 | tf_op jit(solution)/shard_map/gather_blocks/pallas_call | solution.py:674
  125.5 24.5 %attend.1 = (bf16[512,512]{1,0:T(8,128)(2,1)}, f32[4,4,256]{2,1,0:T(4,128)}) custom-call(s32[8]{0:T(128)} %bitcast.106, s32[2]{0:T(128)} %fusion.14.mine_ref, bf16[512,512]{1,0:T(8,128)(2,1)} %get-tuple-element.22.q_ref, bf16[8,256,512]{2,1,0:T(8,128)(2,1)} %bitcast.88, bf16[8,256,512]{2,1,0:T(8,128)(2,1)} %bitcast.104), custom_call_target="tpu_custom_call" | custom-call | flops 8589934592 | bytes 5242880 | tf_op jit(solution)/shard_map/attend/pallas_call | solution.py:82
  153.0 81.2 %scatter_rows.3 = f32[2,64,2048]{2,1,0:T(8,128)S(1)} custom-call(bf16[2,4,64,2048]{3,2,1,0:T(8,128)(2,1)S(1)} %bitcast.85), custom_call_target="tpu_custom_call" | custom-call | bytes 67108864 | tf_op jit(solution)/shard_map/scatter_rows/pallas_call | solution.py:649
  234.6 39.0 %gather_rows.4 = bf16[2,4,64,2048]{3,2,1,0:T(8,128)(2,1)S(1)} custom-call(bf16[2,64,2048]{2,1,0:T(8,128)(2,1)S(1)} %multiply_convert_fusion.5.x_ref), custom_call_target="tpu_custom_call" | custom-call | bytes 67108864 | tf_op jit(solution)/shard_map/gather_rows/pallas_call | solution.py:630
  275.0 15.1 %fusion.22 = f32[512,4096]{1,0:T(8,128)} fusion(bf16[512,2048]{1,0:T(8,128)(2,1)} %bitcast.79, bf16[2048,4096]{1,0:T(8,128)(2,1)} %all-gather.9.cloned.1.call-done), kind=kOutput, calls=%fused_computation.69 | convolution fusion | flops 8589934592 | bytes 27262976 | tf_op jit(solution)/shard_map/dot_general | solution.py:776
  290.1 12.2 %multiply_convert_fusion.1 = (bf16[512,2048]{1,0:T(8,128)(2,1)S(1)}, bf16[512,2048]{1,0:T(8,128)(2,1)}, bf16[512,2048]{1,0:T(8,128)(2,1)}) fusion(f32[512,4096]{1,0:T(8,128)} %fusion.22, bf16[512,2048]{1,0:T(8,128)(2,1)} %bitcast.86, bf16[2048,2048]{1,0:T(8,128)(2,1)} %all-gather.11.cloned.1.call-done), kind=kOutput, calls=%fused_computation.8 | convolution fusion | flops 4311744512 | bytes 25165824 | tf_op jit(solution)/shard_map/dot_general | solution.py:781
  302.3 13.8 %convolution_convert_fusion.7 = bf16[512,2048]{1,0:T(8,128)(2,1)S(1)} fusion(bf16[2048,4096]{1,0:T(8,128)(2,1)} %all-gather.9.cloned.1.call-done, bf16[512,2048]{1,0:T(8,128)(2,1)} %get-tuple-element.53, bf16[512,2048]{1,0:T(8,128)(2,1)S(1)} %get-tuple-element.52), kind=kOutput, calls=%fused_computation.16 | convolution fusion | flops 8599371776 | bytes 23068672 | tf_op jit(solution)/shard_map/dot_general | solution.py:794
  316.1 90.2 %scatter_rows.4 = f32[2,64,2048]{2,1,0:T(8,128)S(1)} custom-call(bf16[2,4,64,2048]{3,2,1,0:T(8,128)(2,1)S(1)} %bitcast.84), custom_call_target="tpu_custom_call" | custom-call | bytes 67108864 | tf_op jit(solution)/shard_map/scatter_rows/pallas_call | solution.py:649
  407.0 61.3 %gather_rows.5 = bf16[2,4,64,2048]{3,2,1,0:T(8,128)(2,1)S(1)} custom-call(bf16[2,64,2048]{2,1,0:T(8,128)(2,1)S(1)} %fusion.13.x_ref), custom_call_target="tpu_custom_call" | custom-call | bytes 67108864 | tf_op jit(solution)/shard_map/gather_rows/pallas_call | solution.py:630
  472.3 10.0 %convolution_convert_fusion.5 = bf16[512,2048]{1,0:T(8,128)(2,1)} fusion(bf16[512,2048]{1,0:T(8,128)(2,1)} %get-tuple-element.54, bf16[2048,2048]{1,0:T(8,128)(2,1)} %all-gather.11.cloned.1.call-done), kind=kOutput, calls=%fused_computation.14 | convolution fusion | flops 4296015872 | bytes 12582912 | tf_op jit(solution)/shard_map/dot_general | solution.py:810
  484.4 41.3 %attend_back.1 = (bf16[512,512]{1,0:T(8,128)(2,1)}, bf16[8,256,512]{2,1,0:T(8,128)(2,1)}, bf16[8,256,512]{2,1,0:T(8,128)(2,1)}) custom-call(s32[8]{0:T(128)} %bitcast.107, s32[2]{0:T(128)} %fusion.14.mine_ref, bf16[512,512]{1,0:T(8,128)(2,1)} %get-tuple-element.22.q_ref, bf16[8,256,512]{2,1,0:T(8,128)(2,1)} %bitcast.89, bf16[8,256,512]{2,1,0:T(8,128)(2,1)} %bitcast.105, ...), custom_call_target="tpu_custom_call" | custom-call | flops 21474836480 | bytes 10485760 | tf_op jit(solution)/shard_map/attend_back/pallas_call | solution.py:178
  527.3 94.0 %scatter_blocks.1 = (f32[2,64,2048]{2,1,0:T(8,128)S(1)}, bf16[512,512]{1,0:T(8,128)(2,1)S(1)}, bf16[512,512]{1,0:T(8,128)(2,1)S(1)}) custom-call(bf16[2,4,64,2048]{3,2,1,0:T(8,128)(2,1)S(1)} %bitcast.76, bf16[4,512,512]{2,1,0:T(8,128)(2,1)} %bitcast.94, bf16[4,512,512]{2,1,0:T(8,128)(2,1)} %bitcast.95), custom_call_target="tpu_custom_call" | custom-call | bytes 67108864 | tf_op jit(solution)/shard_map/scatter_blocks/pallas_call | solution.py:698
  624.4 5.4 convolution_convert_fusion.2
  629.9 10.1 %convolution_convert_fusion.1 = bf16[2048,2048]{1,0:T(8,128)(2,1)} fusion(bf16[512,2048]{1,0:T(8,128)(2,1)} %get-tuple-element.54, bf16[512,2048]{1,0:T(8,128)(2,1)} %bitcast.87), kind=kOutput, calls=%fused_computation.1 | convolution fusion | flops 4299161600 | bytes 12582912 | tf_op jit(solution)/shard_map/dot_general | solution.py:786
  640.2 15.0 %convolution_convert_fusion = bf16[2048,4096]{1,0:T(8,128)(2,1)} fusion(bf16[512,2048]{1,0:T(8,128)(2,1)} %bitcast.80, bf16[512,2048]{1,0:T(8,128)(2,1)} %get-tuple-element.53, bf16[512,2048]{1,0:T(8,128)(2,1)} %copy-done.30), kind=kOutput, calls=%fused_computation | convolution fusion | flops 8606711808 | bytes 23068672 | tf_op jit(solution)/shard_map/dot_general | solution.py:790
  655.2 6.7 convolution_convert_fusion.4
  662.0 90.1 %scatter_rows.5 = f32[2,64,2048]{2,1,0:T(8,128)S(1)} custom-call(bf16[2,4,64,2048]{3,2,1,0:T(8,128)(2,1)S(1)} %bitcast.83), custom_call_target="tpu_custom_call" | custom-call | bytes 67108864 | tf_op jit(solution)/shard_map/scatter_rows/pallas_call | solution.py:649
  762.8 11.8 %reduce-scatter.11.cloned.1.call-done = bf16[2048,256]{1,0:T(8,128)(2,1)} async-done(((bf16[2048,2048]{1,0:T(8,128)(2,1)}), bf16[2048,256]{1,0:T(8,128)(2,1)}) %reduce-scatter.11.cloned.1.call-update) | async-done | bytes 1048592 | tf_op jit(solution)/shard_map/reduce_scatter | solution.py:787
  777.4 117.1 %reduce-scatter.9.cloned.1.call-done = bf16[256,4096]{1,0:T(8,128)(2,1)} async-done(((bf16[2048,4096]{1,0:T(8,128)(2,1)}), bf16[256,4096]{1,0:T(8,128)(2,1)}) %reduce-scatter.9.cloned.1.call-update) | async-done | bytes 2097168 | tf_op jit(solution)/shard_map/reduce_scatter | solution.py:791
  894.4 5.6 convert_multiply_fusion
  900.0 6.6 reshape.166
  906.6 11.7 %psum.7 = f32[2,256]{1,0:T(2,128)S(1)} all-reduce(f32[2,256]{1,0:T(2,128)S(1)} %pad_maximum_fusion.3), channel_id=1, replica_groups=mesh['dp'=2,'ctx'=4,'tp'=4] {'tp'}, use_global_device_ids=true, to_apply=%region_9.10 | all-reduce | flops 512 | bytes 4096 | tf_op jit(solution)/shard_map/psum | solution.py:833
  (124 shorter events, 59.1 us)
Async XLA Ops:
  7.2 62.9 %all-gather.5.cloned.1.call-start = ((), (), s32[]{:S(2)}) async-start(), calls=%async_computation.4 | async-start | bytes 7077888 | tf_op jit(solution)/shard_map/all_gather | solution.py:750
  7.9 4.6 copy-start.22
  12.5 4.6 copy-start.15
  12.5 2.1 copy-start.27
  13.8 136.2 %all-gather.7.cloned.1.call-start = ((), (), s32[]{:S(2)}) async-start(), calls=%async_computation.5 | async-start | bytes 2359296 | tf_op jit(solution)/shard_map/all_gather | solution.py:751
  14.5 260.5 %all-gather.9.cloned.1.call-start = ((), (), s32[]{:S(2)}) async-start(), calls=%async_computation.6 | async-start | bytes 18874368 | tf_op jit(solution)/shard_map/all_gather | solution.py:752
  14.6 2.6 copy-start.24
  20.9 269.1 %all-gather.11.cloned.1.call-start = ((), (), s32[]{:S(2)}) async-start(), calls=%async_computation.7 | async-start | bytes 9437184 | tf_op jit(solution)/shard_map/all_gather | solution.py:755
  21.5 732.6 %reduce-scatter.7.cloned.1.call-start = ((), (), s32[]{:S(2)}) async-start(), calls=%async_computation.9 | async-start | bytes 2359296 | tf_op jit(solution)/shard_map/reduce_scatter | solution.py:807
  22.0 41.3 %copy-start.28 = (s32[1,8]{1,0:T(1,128)S(1)}, s32[1,8]{1,0:T(1,128)}, u32[]{:S(2)}) copy-start(s32[1,8]{1,0:T(1,128)} %param.10) | copy-start | bytes 100
  70.1 8.8 copy-start
  302.3 13.9 %copy-start.30 = (bf16[512,2048]{1,0:T(8,128)(2,1)}, bf16[512,2048]{1,0:T(8,128)(2,1)S(1)}, u32[]{:S(2)}) copy-start(bf16[512,2048]{1,0:T(8,128)(2,1)S(1)} %get-tuple-element.52) | copy-start | bytes 6291460
  407.0 62.6 %copy-start.29 = (bf16[512,512]{1,0:T(8,128)(2,1)S(1)}, bf16[512,512]{1,0:T(8,128)(2,1)}, u32[]{:S(2)}) copy-start(bf16[512,512]{1,0:T(8,128)(2,1)} %get-tuple-element.27.o_ref) | copy-start | bytes 1572868
  472.3 283.7 %reduce-scatter.5.cloned.1.call-start = ((), (), s32[]{:S(2)}) async-start(), calls=%async_computation.8 | async-start | bytes 7077888 | tf_op jit(solution)/shard_map/reduce_scatter | solution.py:820
  472.3 10.1 %copy-start.6 = (bf16[2,4,64,2048]{3,2,1,0:T(8,128)(2,1)S(1)}, bf16[2,4,64,2048]{3,2,1,0:T(8,128)(2,1)}, u32[]{:S(2)}) copy-start(bf16[2,4,64,2048]{3,2,1,0:T(8,128)(2,1)} %copy-done.5) | copy-start | bytes 6291460
  472.3 10.0 %copy-start.26 = (bf16[512,2048]{1,0:T(8,128)(2,1)S(1)}, bf16[512,2048]{1,0:T(8,128)(2,1)}, u32[]{:S(2)}) copy-start(bf16[512,2048]{1,0:T(8,128)(2,1)} %all-gather.7.cloned.1.call-done) | copy-start | bytes 6291460
  527.3 95.0 %copy-start.18 = (bf16[512,512]{1,0:T(8,128)(2,1)S(1)}, bf16[512,512]{1,0:T(8,128)(2,1)}, u32[]{:S(2)}) copy-start(bf16[512,512]{1,0:T(8,128)(2,1)} %get-tuple-element.33) | copy-start | bytes 1572868
  622.3 2.2 copy-start.3
  629.8 144.8 %reduce-scatter.11.cloned.1.call-start = ((), (), s32[]{:S(2)}) async-start(), calls=%async_computation.11 | async-start | bytes 9437184 | tf_op jit(solution)/shard_map/reduce_scatter | solution.py:787
  640.0 254.5 %reduce-scatter.9.cloned.1.call-start = ((), (), s32[]{:S(2)}) async-start(), calls=%async_computation.10 | async-start | bytes 18874368 | tf_op jit(solution)/shard_map/reduce_scatter | solution.py:791
  662.0 90.1 %copy-start.21 = (f32[2,64]{1,0:T(2,128)S(1)}, f32[2,64]{1,0:T(2,128)}, u32[]{:S(2)}) copy-start(f32[2,64]{1,0:T(2,128)} %copy-done.20) | copy-start | bytes 1540
  662.0 90.4 %copy-start.8 = (f32[2,64,2048]{2,1,0:T(8,128)S(1)}, f32[2,64,2048]{2,1,0:T(8,128)}, u32[]{:S(2)}) copy-start(f32[2,64,2048]{2,1,0:T(8,128)} %copy-done.7) | copy-start | bytes 3145732
  752.4 3.5 copy-start.23
  762.8 131.6 %copy-start.25 = (f32[256]{0:T(256)S(1)}, f32[256]{0:T(256)}, u32[]{:S(2)}) copy-start(f32[256]{0:T(256)} %copy-done.24) | copy-start | bytes 3076
  (15 other events, 18.8 us)
Sparse Core Ops, SparseCore 0:
  13.9 48.1 all-gather.4
  63.9 33.8 all-gather.6
  99.7 89.7 all-gather.8
  191.1 55.8 all-gather.10
  472.4 39.9 reduce-scatter.6
  630.0 69.8 reduce-scatter.4
  703.3 71.2 reduce-scatter.10
  778.2 116.1 reduce-scatter.8

commit v2 on v1

v2 whole, which is shorter than its diff:
```python
import functools

import jax
import jax.numpy as jnp
from jax import lax
from jax.experimental import pallas as pl
from jax.experimental.pallas import tpu as pltpu
from jax.sharding import PartitionSpec as P

HEAD_DIM = 64
PAIR = 2 * HEAD_DIM
NT = (((1,), (1,)), ((), ()))
NN = (((1,), (0,)), ((), ()))
TN = (((0,), (0,)), ((), ()))


def dot(a, b, dims):
    return lax.dot_general(a, b, dims, preferred_element_type=jnp.float32)


def swap_halves(x):
    lane = lax.broadcasted_iota(jnp.int32, x.shape, 1)
    half = HEAD_DIM // 2
    return jnp.where(
        lane % HEAD_DIM < half, pltpu.roll(x, PAIR - half, 1), pltpu.roll(x, half, 1)
    )


def head_part(x, head):
    lane = lax.broadcasted_iota(jnp.int32, x.shape, 1)
    return jnp.where(lane // HEAD_DIM == head, x, jnp.zeros_like(x))


def visible(shape, base, key_off, key_id, query_id, span):
    keys = lax.broadcasted_iota(jnp.int32, shape, 0)
    queries = lax.broadcasted_iota(jnp.int32, shape, 1)
    return keys - queries <= (query_id - key_id) * span


def attend_kernel(order_ref, mine_ref, q_ref, k_ref, v_ref, o_ref, lse_ref, s_ref):
    blocks, span, _ = k_ref.shape
    rows = q_ref.shape[0]
    parts = rows // span

    def one(index, carry):
        head = index // parts
        part = index % parts
        start = pl.multiple_of(part * span, span)
        query = head_part(q_ref[pl.ds(start, span), :], head)
        top = jnp.full((8, span), -1e30, jnp.float32)
        for blk in range(blocks):
            s = dot(k_ref[blk], query, NT)
            seen = visible((span, span), 0, 0, order_ref[blk], mine_ref[part], span)
            s = jnp.where(seen, s, -jnp.inf)
            s_ref[blk] = s
            top = jnp.maximum(top, jnp.max(s.reshape(span // 8, 8, span), 0))
        top = jnp.max(top, 0, keepdims=True)
        total = jnp.zeros((8, span), jnp.float32)
        acc = jnp.zeros((PAIR, span), jnp.float32)
        for blk in range(blocks):
            p = jnp.exp(s_ref[blk] - top)
            total = total + jnp.sum(p.reshape(span // 8, 8, span), 0)
            acc = acc + dot(v_ref[blk], p.astype(jnp.bfloat16), TN)
        total = jnp.sum(total, 0, keepdims=True)
        out = (acc / total).T
        lane = lax.broadcasted_iota(jnp.int32, out.shape, 1)
        old = o_ref[pl.ds(start, span), :]
        o_ref[pl.ds(start, span), :] = jnp.where(
            lane // HEAD_DIM == head, out.astype(o_ref.dtype), old
        )
        lse_ref[0, pl.ds(head * parts + part, 1), :] = top + jnp.log(total)
        return carry

    lax.fori_loop(0, 2 * parts, one, 0)


def attend(order, mine, q, k, v):
    rows, width = q.shape
    blocks, span, _ = k.shape
    pairs = width // PAIR
    parts = rows // span
    return pl.pallas_call(
        attend_kernel,
        out_shape=(
            jax.ShapeDtypeStruct((rows, width), jnp.bfloat16),
            jax.ShapeDtypeStruct((pairs, 2 * parts, span), jnp.float32),
        ),
        grid_spec=pltpu.PrefetchScalarGridSpec(
            num_scalar_prefetch=2,
            grid=(pairs,),
            in_specs=[
                pl.BlockSpec((rows, PAIR), lambda i, *_: (0, i)),
                pl.BlockSpec((blocks, span, PAIR), lambda i, *_: (0, 0, i)),
                pl.BlockSpec((blocks, span, PAIR), lambda i, *_: (0, 0, i)),
            ],
            out_specs=[
                pl.BlockSpec((rows, PAIR), lambda i, *_: (0, i)),
                pl.BlockSpec((1, 2 * parts, span), lambda i, *_: (i, 0, 0)),
            ],
            scratch_shapes=[pltpu.VMEM((blocks, span, span), jnp.float32)],
        ),
        cost_estimate=pl.CostEstimate(
            flops=4 * rows * blocks * span * width * 4,
            bytes_accessed=4 * blocks * span * width + 4 * rows * width,
            transcendentals=rows * blocks * span * width // HEAD_DIM,
        ),
        name="attend",
    )(order, mine, q, k, v)


def attend_back_kernel(
    order_ref, mine_ref, q_ref, k_ref, v_ref, o_ref, g_ref, lse_ref, cos_ref, sin_ref,
    qcos_ref, qsin_ref, dq_ref, dk_ref, dv_ref, dk_acc, dv_acc, dq_acc, kt_ref, delta_ref,
):
    blocks, span, _ = k_ref.shape
    rows = q_ref.shape[0]
    parts = rows // span
    f32 = jnp.float32
    bf16 = jnp.bfloat16
    for blk in range(blocks):
        kt_ref[blk] = k_ref[blk].T
        dk_acc[blk] = jnp.zeros((span, PAIR), f32)
        dv_acc[blk] = jnp.zeros((span, PAIR), f32)
    for part in range(parts):
        take = pl.ds(part * span, span)
        both = (g_ref[take, :].astype(f32) * o_ref[take, :].astype(f32)).T
        for head in range(2):
            delta_ref[pl.ds(head * parts + part, 1), :] = jnp.sum(
                both[head * HEAD_DIM : (head + 1) * HEAD_DIM], 0, keepdims=True
            )
        dq_acc[part] = jnp.zeros((PAIR, span), f32)

    def one(index, carry):
        head = index // parts
        part = index % parts
        start = pl.multiple_of(part * span, span)
        query = head_part(q_ref[pl.ds(start, span), :], head)
        grad = head_part(g_ref[pl.ds(start, span), :], head)
        lse = lse_ref[0, pl.ds(index, 1), :]
        delta = delta_ref[pl.ds(index, 1), :]
        dq = jnp.zeros((PAIR, span), f32)
        for blk in range(blocks):
            s = dot(k_ref[blk], query, NT)
            seen = visible((span, span), 0, 0, order_ref[blk], mine_ref[part], span)
            p = jnp.exp(jnp.where(seen, s - lse, -jnp.inf))
            dp = dot(v_ref[blk], grad, NT)
            ds = (p * (dp - delta)).astype(bf16)
            dv_acc[blk] += dot(p.astype(bf16), grad, NN)
            dk_acc[blk] += dot(ds, query, NN)
            dq = dq + dot(kt_ref[blk], ds, NN)
        sub = lax.broadcasted_iota(jnp.int32, dq.shape, 0)
        dq_acc[part] += jnp.where(sub // HEAD_DIM == head, dq, 0.0)
        return carry

    lax.fori_loop(0, 2 * parts, one, 0)
    for part in range(parts):
        take = pl.ds(part * span, span)
        dq = dq_acc[part].T
        dq = dq * qcos_ref[take, :] - swap_halves(dq) * qsin_ref[take, :]
        dq_ref[take, :] = (dq * 0.125).astype(bf16)
    for blk in range(blocks):
        dk = dk_acc[blk]
        dk = dk * cos_ref[blk] - swap_halves(dk) * sin_ref[blk]
        dk_ref[blk] = dk.astype(bf16)
        dv_ref[blk] = dv_acc[blk].astype(bf16)


def attend_back(order, mine, q, k, v, o, g, lse, cos, sin, qcos, qsin):
    rows, width = q.shape
    blocks, span, _ = k.shape
    pairs = width // PAIR
    parts = rows // span
    row_spec = pl.BlockSpec((rows, PAIR), lambda i, *_: (0, i))
    blk_spec = pl.BlockSpec((blocks, span, PAIR), lambda i, *_: (0, 0, i))
    tab_spec = pl.BlockSpec((blocks, span, PAIR), lambda i, *_: (0, 0, 0))
    qtab_spec = pl.BlockSpec((rows, PAIR), lambda i, *_: (0, 0))
    f32 = jnp.float32
    return pl.pallas_call(
        attend_back_kernel,
        out_shape=(
            jax.ShapeDtypeStruct((rows, width), jnp.bfloat16),
            jax.ShapeDtypeStruct((blocks, span, width), jnp.bfloat16),
            jax.ShapeDtypeStruct((blocks, span, width), jnp.bfloat16),
        ),
        grid_spec=pltpu.PrefetchScalarGridSpec(
            num_scalar_prefetch=2,
            grid=(pairs,),
            in_specs=[
                row_spec, blk_spec, blk_spec, row_spec, row_spec,
                pl.BlockSpec((1, 2 * parts, span), lambda i, *_: (i, 0, 0)),
                tab_spec, tab_spec, qtab_spec, qtab_spec,
            ],
            out_specs=[row_spec, blk_spec, blk_spec],
            scratch_shapes=[
                pltpu.VMEM((blocks, span, PAIR), f32),
                pltpu.VMEM((blocks, span, PAIR), f32),
                pltpu.VMEM((parts, PAIR, span), f32),
                pltpu.VMEM((blocks, PAIR, span), jnp.bfloat16),
                pltpu.VMEM((2 * parts, span), f32),
            ],
        ),
        cost_estimate=pl.CostEstimate(
            flops=10 * rows * blocks * span * width * 4,
            bytes_accessed=8 * blocks * span * width + 8 * rows * width,
            transcendentals=rows * blocks * span * width // HEAD_DIM,
        ),
        name="attend_back",
    )(order, mine, q, k, v, o, g, lse, cos, sin, qcos, qsin)


def project_kernel(x_ref, w_ref, cos_ref, sin_ref, q_ref, k_ref, v_ref):
    which = pl.program_id(0)
    out = dot(x_ref[...], w_ref[...], NN)

    def turned(scale, ref):
        for lane in range(0, out.shape[1], PAIR):
            piece = out[:, lane : lane + PAIR]
            piece = piece * cos_ref[...] + swap_halves(piece) * sin_ref[...]
            ref[:, lane : lane + PAIR] = (piece * scale).astype(ref.dtype)

    @pl.when(which == 0)
    def _():
        turned(0.125, q_ref)

    @pl.when(which == 1)
    def _():
        turned(1.0, k_ref)

    @pl.when(which == 2)
    def _():
        v_ref[...] = out.astype(v_ref.dtype)


def project(x, w, qcos, qsin):
    rows, depth = x.shape
    width = w.shape[1] // 3
    whole = lambda shape: pl.BlockSpec(shape, lambda t: (0,) * len(shape))
    out = jax.ShapeDtypeStruct((rows, width), jnp.bfloat16)
    return pl.pallas_call(
        project_kernel,
        out_shape=(out, out, out),
        grid=(3,),
        in_specs=[
            whole((rows, depth)),
            pl.BlockSpec((depth, width), lambda t: (0, t)),
            whole((rows, PAIR)),
            whole((rows, PAIR)),
        ],
        out_specs=[whole((rows, width))] * 3,
        cost_estimate=pl.CostEstimate(
            flops=2 * rows * depth * 3 * width,
            bytes_accessed=2 * depth * 3 * width + 2 * rows * depth,
            transcendentals=0,
        ),
        name="project",
    )(x, w, qcos, qsin)


def cube_size(axes):
    size = 1
    for axis in axes:
        size *= lax.axis_size(axis)
    return size


def cube_index(axes):
    index = 0
    for axis in axes:
        index = index * lax.axis_size(axis) + lax.axis_index(axis)
    return index


def cube_bits(size):
    bits = []
    while size > 1:
        size //= 2
        bits.append(size)
    return bits


def flipped(index, bit):
    return index + bit - 2 * bit * ((index // bit) % 2)


def flip_all(index, mask):
    bit = 1
    while bit <= mask:
        if mask // bit % 2:
            index = flipped(index, bit)
        bit *= 2
    return index


def cube_peer(axes, bit):
    for axis in axes[::-1]:
        size = lax.axis_size(axis)
        if bit < size:
            return {axis: flipped(lax.axis_index(axis), bit)}
        bit //= size
    raise ValueError(bit)


def greet(line_axis, cube_axes):
    sem = pltpu.get_barrier_semaphore()
    count = 0

    def hello(target):
        pl.semaphore_signal(sem, inc=1, device_id=target, device_id_type=MESH)

    if line_axis is not None:
        me = lax.axis_index(line_axis)
        size = lax.axis_size(line_axis)

        @pl.when(me > 0)
        def _():
            hello({line_axis: me - 1})

        @pl.when(me < size - 1)
        def _():
            hello({line_axis: me + 1})

    if cube_axes is not None:
        for bit in cube_bits(cube_size(cube_axes)):
            hello(cube_peer(cube_axes, bit))
            count += 1
    if line_axis is not None:

        @pl.when((me > 0) & (me < size - 1))
        def _():
            pl.semaphore_wait(sem, count + 2)

        @pl.when((me == 0) | (me == size - 1))
        def _():
            pl.semaphore_wait(sem, count + 1)

    else:
        pl.semaphore_wait(sem, count)


def remote(src, dst, send, recv, target):
    return pltpu.make_async_remote_copy(
        src_ref=src, dst_ref=dst, send_sem=send, recv_sem=recv,
        device_id=target, device_id_type=MESH,
    )


class RowGather:
    def __init__(self, axis, x_ref, o_ref, send, recv, local):
        self.axis, self.x, self.o = axis, x_ref, o_ref
        self.send, self.recv, self.local = send, recv, local
        self.size = lax.axis_size(axis)
        self.me = lax.axis_index(axis)
        self.pieces = x_ref.shape[0]

    @staticmethod
    def scratch(size, pieces):
        return [
            pltpu.SemaphoreType.DMA((2, size - 1, pieces)),
            pltpu.SemaphoreType.DMA((2, size - 1, pieces)),
            pltpu.SemaphoreType.DMA((pieces,)),
        ]

    def peer(self, way):
        return {self.axis: self.me + 1 if way == 0 else self.me - 1}

    def own(self, p):
        return pltpu.make_async_copy(self.x.at[p], self.o.at[p, self.me], self.local.at[p])

    def copy(self, way, step, p):
        block = self.me - step if way == 0 else self.me + step
        src = self.x.at[p] if step == 0 else self.o.at[p, block]
        return remote(
            src, self.o.at[p, block], self.send.at[way, step, p], self.recv.at[way, step, p],
            self.peer(way),
        )

    def sends(self, way, step):
        if way == 0:
            return (self.me < self.size - 1) & (self.me - step >= 0)
        return (self.me > 0) & (self.me + step < self.size)

    def arrives(self, way, step):
        return self.me - 1 - step >= 0 if way == 0 else self.me + 1 + step < self.size

    def arrival(self, way, step, p):
        block = self.me - 1 - step if way == 0 else self.me + 1 + step
        return remote(
            self.o.at[p, block], self.o.at[p, block], self.send.at[way, step, p],
            self.recv.at[way, step, p], self.peer(1 - way),
        )

    def start(self, p):
        for way in (0, 1):

            @pl.when(self.sends(way, 0))
            def _(way=way):
                self.copy(way, 0, p).start()

        self.own(p).start()

    def flow(self):
        for step in range(1, self.size):
            for p in range(self.pieces):
                for way in (0, 1):

                    @pl.when(self.arrives(way, step - 1))
                    def _(way=way, p=p):
                        self.arrival(way, step - 1, p).wait_recv()

                    if step < self.size - 1:

                        @pl.when(self.sends(way, step))
                        def _(way=way, p=p):
                            self.copy(way, step, p).start()

            yield
        for p in range(self.pieces):
            self.own(p).wait()
        for step in range(self.size - 1):
            for way in (0, 1):

                @pl.when(self.sends(way, step))
                def _(way=way, step=step):
                    for p in range(self.pieces):
                        self.copy(way, step, p).wait_send()

    def steps(self):
        for p in range(self.pieces):
            self.start(p)
        yield
        yield from self.flow()


class RowScatter:
    def __init__(self, axis, part_ref, inbox, outbox, send, recv):
        self.axis, self.part, self.inbox, self.outbox = axis, part_ref, inbox, outbox
        self.send, self.recv = send, recv
        self.size = lax.axis_size(axis)
        self.me = lax.axis_index(axis)
        self.pieces = part_ref.shape[0]

    @staticmethod
    def scratch(size, block):
        return [
            pltpu.VMEM((2, size - 1) + block, jnp.bfloat16),
            pltpu.VMEM((2, size - 1) + block, jnp.bfloat16),
            pltpu.SemaphoreType.DMA((2, size - 1, block[0])),
            pltpu.SemaphoreType.DMA((2, size - 1, block[0])),
        ]

    def peer(self, way):
        return {self.axis: self.me + 1 if way == 0 else self.me - 1}

    def target(self, way, step):
        return self.size - 1 - step if way == 0 else step

    def edge(self, way):
        return self.me == 0 if way == 0 else self.me == self.size - 1

    def inner(self, way):
        return self.me > 0 if way == 0 else self.me < self.size - 1

    def passes(self, way, step):
        dest = self.target(way, step)
        return dest > self.me if way == 0 else dest < self.me

    def copy(self, way, step, p, edge):
        src = self.part.at[p, self.target(way, step)] if edge else self.outbox.at[way, step, p]
        return remote(
            src, self.inbox.at[way, step, p], self.send.at[way, step, p],
            self.recv.at[way, step, p], self.peer(way),
        )

    def arrival(self, way, step, p):
        return remote(
            self.inbox.at[way, step, p], self.inbox.at[way, step, p],
            self.send.at[way, step, p], self.recv.at[way, step, p], self.peer(1 - way),
        )

    def flow(self):
        f32 = jnp.float32
        for way in (0, 1):

            @pl.when(self.edge(way))
            def _(way=way):
                for step in range(self.size - 1):
                    for p in range(self.pieces):
                        self.copy(way, step, p, True).start()

        yield
        for step in range(self.size - 1):
            for p in range(self.pieces):
                for way in (0, 1):

                    @pl.when(self.passes(way, step) & self.inner(way))
                    def _(way=way, step=step, p=p):
                        self.arrival(way, step, p).wait_recv()
                        self.outbox[way, step, p] = (
                            self.inbox[way, step, p].astype(f32)
                            + self.part[p, self.target(way, step)].astype(f32)
                        ).astype(self.outbox.dtype)
                        self.copy(way, step, p, False).start()

            yield

    def collect(self, p, o_ref):
        f32 = jnp.float32
        o_ref[p] = self.part[p, self.me].astype(f32)
        for way in (0, 1):

            @pl.when(self.inner(way))
            def _(way=way):
                step = self.size - 1 - self.me if way == 0 else self.me
                self.arrival(way, step, p).wait_recv()
                o_ref[p] += self.inbox[way, step, p].astype(f32)

    def finish(self):
        for step in range(self.size - 1):
            for way in (0, 1):

                @pl.when(self.passes(way, step))
                def _(way=way, step=step):
                    for p in range(self.pieces):
                        self.copy(way, step, p, False).wait_send()

    def steps(self, o_ref):
        yield from self.flow()
        for p in range(self.pieces):
            self.collect(p, o_ref)
        yield
        self.finish()


def cube_gather_steps(axes, count, source, place, send, recv, local):
    size = cube_size(axes)
    me = cube_index(axes)
    bits = cube_bits(size)
    own = [
        pltpu.make_async_copy(source(t), place(t, me), local.at[t]) for t in range(count)
    ]

    def copy(mask, bit, t):
        block = flip_all(me, mask)
        src = source(t) if mask == 0 else place(t, block)
        return remote(
            src, place(t, block), send.at[mask + bit, t], recv.at[mask + bit, t],
            cube_peer(axes, bit),
        )

    def arrival(mask, t):
        place_here = place(t, flip_all(me, mask))
        return remote(
            place_here, place_here, send.at[mask, t], recv.at[mask, t],
            cube_peer(axes, mask & -mask),
        )

    for bit in bits:
        for t in range(count):
            copy(0, bit, t).start()
    for one in own:
        one.start()
    yield
    waited = set()
    masks = [0]
    for bit in bits:
        for mask in masks:
            if mask == 0:
                continue
            for t in range(count):
                if (mask, t) not in waited:
                    arrival(mask, t).wait_recv()
                    waited.add((mask, t))
                copy(mask, bit, t).start()
            yield
        masks = masks + [mask + bit for mask in masks]
    for mask in masks:
        for t in range(count):
            if mask and (mask, t) not in waited:
                arrival(mask, t).wait_recv()
    for one in own:
        one.wait()
    for mask in masks:
        for t in range(count):
            if mask:
                low = mask & -mask
                copy(mask - low, low, t).wait_send()


def cube_gather_scratch(size, count):
    return [
        pltpu.SemaphoreType.DMA((size, count)),
        pltpu.SemaphoreType.DMA((size, count)),
        pltpu.SemaphoreType.DMA((count,)),
    ]


def cube_scatter_steps(axes, parts, inbox, total, outbox, send, recv, done):
    size = cube_size(axes)
    me = cube_index(axes)
    bits = cube_bits(size)[::-1]
    count = len(parts)
    f32 = jnp.float32
    order = sorted(range(size), key=lambda mask: tuple(-(mask & bit) for bit in bits))

    def copy(mask, t):
        bit = mask & -mask
        src = parts[t].at[flip_all(me, mask)] if bit == 1 else outbox.at[mask // 2, t]
        return remote(
            src, inbox.at[mask, t], send.at[mask, t], recv.at[mask, t], cube_peer(axes, bit)
        )

    for mask in order:
        if mask & 1:
            for t in range(count):
                copy(mask, t).start()
    yield
    for level, bit in enumerate(bits):
        after = bits[level + 1] if level + 1 < len(bits) else 0
        for mask in order:
            if mask % (2 * bit):
                continue
            for t in range(count):
                copy(mask + bit, t).wait_recv()
                if bit == 1:
                    base = parts[t][flip_all(me, mask)].astype(f32)
                else:
                    base = total[mask // 4, t]
                value = base + inbox[mask + bit, t].astype(f32)
                if mask & after:
                    outbox[mask // 2, t] = value.astype(outbox.dtype)
                    copy(mask, t).start()
                elif after:
                    total[mask // 4, t] = value
                else:
                    done(t, value)
            yield
    for mask in range(1, size):
        for t in range(count):
            copy(mask, t).wait_send()


def cube_scatter_scratch(size, block, count):
    return [
        pltpu.VMEM((size, count) + block, jnp.bfloat16),
        pltpu.VMEM((max(size // 4, 1), count) + block, jnp.float32),
        pltpu.VMEM((max(size // 2, 1), count) + block, jnp.bfloat16),
        pltpu.SemaphoreType.DMA((size, count)),
        pltpu.SemaphoreType.DMA((size, count)),
    ]


def run_steps(walks, order=()):
    walks = list(walks)
    for index in order:
        next(walks[index], None)
    while walks:
        for walk in list(walks):
            try:
                next(walk)
            except StopIteration:
                walks.remove(walk)


ANY = pl.BlockSpec(memory_space=pl.ANY)
IN_VMEM = pl.BlockSpec(memory_space=pltpu.VMEM)


def comm_call(kernel, number, size, **kwargs):
    return pl.pallas_call(
        kernel,
        compiler_params=pltpu.CompilerParams(
            collective_id=number, has_side_effects=True, vmem_limit_bytes=52 * 1024 * 1024
        ),
        cost_estimate=pl.CostEstimate(flops=0, bytes_accessed=size, transcendentals=0),
        **kwargs,
    )


def enter(x, w, number):
    pieces, rows, depth = x.shape
    size = lax.axis_size("tp")
    shards = ("dp", "ctx")
    group = cube_size(shards)
    cuts = 2
    part = w.shape[0] // cuts

    def kernel(x_ref, w_ref, o_ref, wo_ref, *sems):
        greet("tp", shards)
        take = lambda t: pl.ds(t * part, part)
        run_steps(
            (
                RowGather("tp", x_ref, o_ref, *sems[:3]).steps(),
                cube_gather_steps(
                    shards, cuts, lambda t: w_ref.at[take(t)],
                    lambda t, block: wo_ref.at[block, take(t)], *sems[3:],
                ),
            )
        )

    return comm_call(
        kernel, number, COMM_BYTES,
        out_shape=(
            jax.ShapeDtypeStruct((pieces, size, rows, depth), x.dtype),
            jax.ShapeDtypeStruct((group,) + w.shape, w.dtype),
        ),
        in_specs=[IN_VMEM] * 2,
        out_specs=[ANY] * 2,
        scratch_shapes=RowGather.scratch(size, pieces) + cube_gather_scratch(group, cuts),
        name="enter",
    )(x, w)


def gather_blocks(x, keys, values, number):
    pieces, rows, depth = x.shape
    size = lax.axis_size("tp")
    ring = lax.axis_size("ctx")

    def kernel(x_ref, k_ref, v_ref, o_ref, ko_ref, vo_ref, *sems):
        greet("tp", ("ctx",))
        ins, outs = (k_ref, v_ref), (ko_ref, vo_ref)
        run_steps(
            (
                cube_gather_steps(
                    ("ctx",), 2, lambda t: ins[t], lambda t, block: outs[t].at[block], *sems[3:]
                ),
                RowGather("tp", x_ref, o_ref, *sems[:3]).steps(),
            )
        )

    blocks = jax.ShapeDtypeStruct((ring,) + keys.shape, keys.dtype)
    return comm_call(
        kernel, number, COMM_BYTES,
        out_shape=(jax.ShapeDtypeStruct((pieces, size, rows, depth), x.dtype), blocks, blocks),
        in_specs=[IN_VMEM] * 3,
        out_specs=[ANY] * 3,
        scratch_shapes=RowGather.scratch(size, pieces) + cube_gather_scratch(ring, 2),
        name="gather_blocks",
    )(x, keys, values)


def mix_rows(part, sides, finish, number, name):
    pieces, size, rows, depth = part.shape
    count = len(sides)

    def kernel(part_ref, *refs):
        side_refs, (sum_ref, o_ref), refs = refs[:count], refs[count : count + 2], refs[count + 2 :]
        own_ref, scatter_scratch, sems = refs[0], refs[1:5], refs[5:]
        greet("tp", None)
        scatter = RowScatter("tp", part_ref, *scatter_scratch)
        gather = RowGather("tp", own_ref, o_ref, *sems)
        run_steps((scatter.flow(),))
        for p in range(pieces):
            scatter.collect(p, sum_ref)
            kept, sent = finish(sum_ref[p], *(ref[p] for ref in side_refs))
            sum_ref[p] = kept
            own_ref[p] = sent.astype(own_ref.dtype)
            gather.start(p)
        run_steps((gather.flow(),))
        scatter.finish()

    return comm_call(
        kernel, number, 2 * COMM_BYTES,
        out_shape=(
            jax.ShapeDtypeStruct((pieces, rows, depth), jnp.float32),
            jax.ShapeDtypeStruct((pieces, size, rows, depth), jnp.bfloat16),
        ),
        in_specs=[IN_VMEM] * (1 + count),
        out_specs=[IN_VMEM, ANY],
        scratch_shapes=[pltpu.VMEM((pieces, rows, depth), jnp.bfloat16)]
        + RowScatter.scratch(size, (pieces, rows, depth))
        + RowGather.scratch(size, pieces),
        name=name,
    )(part, *sides)


def scatter_blocks(part, dk, dv, number):
    pieces, size, rows, depth = part.shape
    ring = dk.shape[0]

    def kernel(part_ref, k_ref, v_ref, o_ref, ko_ref, vo_ref, *scratch):
        greet("tp", ("ctx",))
        outs = (ko_ref, vo_ref)

        def done(t, value):
            outs[t][...] = value.astype(outs[t].dtype)

        run_steps(
            (
                RowScatter("tp", part_ref, *scratch[:4]).steps(o_ref),
                cube_scatter_steps(("ctx",), (k_ref, v_ref), *scratch[4:], done),
            ),
            (0, 1, 1, 1, 0, 0),
        )

    block = jax.ShapeDtypeStruct(dk.shape[1:], jnp.bfloat16)
    return comm_call(
        kernel, number, COMM_BYTES,
        out_shape=(jax.ShapeDtypeStruct((pieces, rows, depth), jnp.float32), block, block),
        in_specs=[IN_VMEM] * 3,
        out_specs=[IN_VMEM] * 3,
        scratch_shapes=RowScatter.scratch(size, (pieces, rows, depth))
        + cube_scatter_scratch(ring, dk.shape[1:], 2),
        name="scatter_blocks",
    )(part, dk, dv)


def leave(part, grad, number):
    pieces, size, rows, depth = part.shape
    shards = ("dp", "ctx")
    group = cube_size(shards)
    block = grad.shape[1:]

    def kernel(part_ref, g_ref, o_ref, go_ref, *scratch):
        greet("tp", shards)

        def done(t, value):
            go_ref[...] = value

        run_steps(
            (
                RowScatter("tp", part_ref, *scratch[:4]).steps(o_ref),
                cube_scatter_steps(shards, (g_ref,), *scratch[4:], done),
            ),
            (0,) + (1,) * (1 + group // 2) + (0, 0, 1),
        )

    return comm_call(
        kernel, number, COMM_BYTES,
        out_shape=(
            jax.ShapeDtypeStruct((pieces, rows, depth), jnp.float32),
            jax.ShapeDtypeStruct(block, jnp.float32),
        ),
        in_specs=[IN_VMEM] * 2,
        out_specs=[IN_VMEM] * 2,
        scratch_shapes=RowScatter.scratch(size, (pieces, rows, depth))
        + cube_scatter_scratch(group, block, 1),
        name="leave",
    )(part, grad)


def sum_small(x, number):
    size = lax.axis_size("tp")

    def kernel(x_ref, o_ref, inbox, send, recv):
        me = lax.axis_index("tp")
        sem = pltpu.get_barrier_semaphore()
        for step in range(1, size):
            pl.semaphore_signal(
                sem, inc=1, device_id={"tp": (me + step) % size}, device_id_type=MESH
            )
        pl.semaphore_wait(sem, size - 1)
        copies = [
            remote(
                x_ref, inbox.at[step - 1], send.at[step - 1], recv.at[step - 1],
                {"tp": (me + step) % size},
            )
            for step in range(1, size)
        ]
        for copy in copies:
            copy.start()
        total = x_ref[...]
        for step, copy in enumerate(copies):
            copy.wait()
            total = total + inbox[step]
        o_ref[...] = total

    return comm_call(
        kernel, number, x.size * 4,
        out_shape=jax.ShapeDtypeStruct(x.shape, x.dtype),
        in_specs=[IN_VMEM],
        out_specs=IN_VMEM,
        scratch_shapes=[
            pltpu.VMEM((size - 1,) + x.shape, x.dtype),
            pltpu.SemaphoreType.DMA((size - 1,)),
            pltpu.SemaphoreType.DMA((size - 1,)),
        ],
        name="sum_small",
    )(x)


EPSILON = 1e-05
ROPE_BASE = 130000.0
COMM_BYTES = 128 * 1024 * 1024
MESH = pl.DeviceIdType.MESH


def rope_tables(positions):
    half = HEAD_DIM // 2
    lane = jnp.arange(PAIR, dtype=jnp.int32)
    freq = ROPE_BASE ** (-((lane % half).astype(jnp.float32) * 2.0 / HEAD_DIM))
    angle = positions.astype(jnp.float32)[..., None] * freq
    sign = jnp.where(lane % HEAD_DIM < half, -1.0, 1.0)
    return jnp.cos(angle), jnp.sin(angle) * sign


def body(block_input, block_order, w_qkv, w_out, gain_attn, w_gate_up, w_down, gain_mlp, cotangent):
    f32 = jnp.float32
    bf16 = jnp.bfloat16
    shards = ("dp", "ctx")
    _, pieces, row_count, depth = block_input.shape
    span = row_count * lax.axis_size("tp")
    width = w_qkv.shape[2]
    units = w_gate_up.shape[2]
    shard = w_qkv.shape[0]
    rows = pieces * span
    block_total = block_order.shape[1]
    order = block_order[0]
    first = lax.axis_index("ctx") * pieces
    mine = lax.dynamic_slice_in_dim(order, first, pieces, 0)
    offsets = jnp.arange(span, dtype=jnp.int32)
    cos, sin = rope_tables(order[:, None] * span + offsets)
    qcos, qsin = (
        lax.dynamic_slice_in_dim(t, first, pieces, 0).reshape(rows, PAIR) for t in (cos, sin)
    )

    gain_one = gain_attn.astype(f32)[:, None]
    gain_two = gain_mlp.astype(f32)[:, None]
    flat_qkv = w_qkv.reshape(shard, 3 * width).astype(f32)
    flat_gate_up = w_gate_up.reshape(shard, 2 * units).astype(f32)
    x = block_input[0].astype(f32)
    rms_attn = lax.rsqrt(jnp.mean(x * x, -1, keepdims=True) + EPSILON)
    unit_attn = x * rms_attn
    unit_attn_full, full_qkv = enter(
        unit_attn.astype(bf16), (flat_qkv * gain_one).astype(bf16), 0
    )
    unit_attn_full = unit_attn_full.reshape(rows, depth)
    full_qkv = full_qkv.reshape(depth, 3 * width)
    own_out, own_gate_up, own_down, unit_attn_full = lax.optimization_barrier(
        (w_out, (flat_gate_up * gain_two).astype(bf16), w_down, unit_attn_full)
    )
    full_out = lax.all_gather(own_out, shards, axis=1, tiled=True)
    full_gate_up = lax.all_gather(own_gate_up, shards, axis=0, tiled=True)
    full_down = lax.all_gather(own_down, shards, axis=1, tiled=True)
    queries, keys, values = project(unit_attn_full, full_qkv, qcos, qsin)
    cotan_full, key_blocks, value_blocks = gather_blocks(cotangent[0], keys, values, 1)
    cotan_full = cotan_full.reshape(rows, depth)
    key_blocks = key_blocks.reshape(block_total, span, width)
    value_blocks = value_blocks.reshape(block_total, span, width)
    attention, lse = attend(order, mine, queries, key_blocks, value_blocks)

    def spread(part):
        return part.astype(bf16).reshape(pieces, -1, row_count, depth)

    attn_part = jnp.dot(attention, full_out, preferred_element_type=f32)

    def norm_mlp(total, own):
        resid = own.astype(f32) + total
        return resid, resid * lax.rsqrt(jnp.mean(resid * resid, -1, keepdims=True) + EPSILON)

    resid_mid, unit_mlp_full = mix_rows(
        spread(attn_part), (block_input[0],), norm_mlp, 2, "mix_forward"
    )
    unit_mlp_full = unit_mlp_full.reshape(rows, depth)
    gate_up = jnp.dot(unit_mlp_full, full_gate_up, preferred_element_type=f32)
    gate = gate_up[:, :units]
    upper = gate_up[:, units:]
    sigma = jax.nn.sigmoid(gate)
    hidden = (gate * sigma * upper).astype(bf16)
    grad_hidden = lax.dot_general(cotan_full, full_down, NT, preferred_element_type=f32)
    act_grad = jnp.concatenate(
        [grad_hidden * upper * sigma * (1.0 + gate * (1.0 - sigma)), grad_hidden * gate * sigma],
        axis=1,
    ).astype(bf16)
    grad_down_local = lax.dot_general(
        hidden, cotan_full, TN, preferred_element_type=f32
    ).astype(bf16)
    share_down = lax.psum_scatter(grad_down_local, shards, scatter_dimension=1, tiled=True)
    grad_gate_up_local = lax.dot_general(
        unit_mlp_full, act_grad, TN, preferred_element_type=f32
    ).astype(bf16)
    share_gate_up = lax.psum_scatter(grad_gate_up_local, shards, scatter_dimension=0, tiled=True)
    scaled_part = lax.dot_general(act_grad, full_gate_up, NT, preferred_element_type=f32)
    scaled_part, _, _ = lax.optimization_barrier(
        (spread(scaled_part), grad_down_local, grad_gate_up_local)
    )

    def norm_back(total, resid, own):
        rms = lax.rsqrt(jnp.mean(resid * resid, -1, keepdims=True) + EPSILON)
        unit = resid * rms
        grad = own.astype(f32) + rms * (total - unit * jnp.mean(total * unit, -1, keepdims=True))
        return grad, grad

    grad_mid, mid_full = mix_rows(
        scaled_part, (resid_mid, cotangent[0]), norm_back, 3, "mix_backward"
    )
    mid_full = mid_full.reshape(rows, depth)
    grad_attention = lax.dot_general(mid_full, full_out, NT, preferred_element_type=f32)
    grad_queries, key_terms, value_terms = attend_back(
        order, mine, queries, key_blocks, value_blocks, attention, grad_attention.astype(bf16),
        lse, cos, sin, qcos, qsin,
    )
    grad_out_local = lax.dot_general(attention, mid_full, TN, preferred_element_type=f32)
    share_out = lax.psum_scatter(
        grad_out_local.astype(bf16), shards, scatter_dimension=1, tiled=True
    )
    down_part = jnp.dot(hidden, full_down, preferred_element_type=f32)
    down_sum, grad_keys, grad_values = scatter_blocks(
        spread(down_part),
        key_terms.reshape(-1, rows, width),
        value_terms.reshape(-1, rows, width),
        4,
    )
    block_output = (resid_mid + down_sum).astype(bf16)
    qkv_grad = jnp.concatenate([grad_queries, grad_keys, grad_values], axis=1)
    grad_qkv_local = lax.dot_general(unit_attn_full, qkv_grad, TN, preferred_element_type=f32)
    scaled_one_part = lax.dot_general(qkv_grad, full_qkv, NT, preferred_element_type=f32)
    scaled_one, raw_qkv = leave(
        spread(scaled_one_part), grad_qkv_local.astype(bf16).reshape(-1, shard, 3 * width), 5
    )
    input_grad = grad_mid + rms_attn * (
        scaled_one - unit_attn * jnp.mean(scaled_one * unit_attn, -1, keepdims=True)
    )
    raw_gate_up = share_gate_up.astype(f32)
    gain_terms = jnp.stack(
        [jnp.sum(raw_qkv * flat_qkv, -1), jnp.sum(raw_gate_up * flat_gate_up, -1)]
    )
    gain_sums = sum_small(gain_terms, 6)
    return (
        block_output[None],
        input_grad[None],
        (raw_qkv * gain_one).reshape(shard, 3, width),
        share_out.astype(f32),
        gain_sums[0],
        (raw_gate_up * gain_two).reshape(shard, 2, units),
        share_down.astype(f32),
        gain_sums[1],
    )


def solution(mesh):
    in_specs = (
        P("dp", "ctx", "tp", None),
        P("dp", None),
        P(("dp", "ctx"), None, "tp"),
        P("tp", ("dp", "ctx")),
        P(("dp", "ctx")),
        P(("dp", "ctx"), None, "tp"),
        P("tp", ("dp", "ctx")),
        P(("dp", "ctx")),
        P("dp", "ctx", "tp", None),
    )
    out_specs = (
        P("dp", "ctx", "tp", None),
        P("dp", "ctx", "tp", None),
        P(("dp", "ctx"), None, "tp"),
        P("tp", ("dp", "ctx")),
        P(("dp", "ctx")),
        P(("dp", "ctx"), None, "tp"),
        P("tp", ("dp", "ctx")),
        P(("dp", "ctx")),
    )
    return jax.shard_map(body, mesh=mesh, in_specs=in_specs, out_specs=out_specs, check_vma=False)
```

time: 935 us -> 675 us (0.72)
  Pallas kernels: 611 us -> 427 us
  waiting for transfers between devices: 130 us -> 72.1 us
  blocking collectives: 11.7 us -> 0 us
    pallas_call x8 -> x7, Pallas kernels: 537 us -> 352 us  [the longest x2 144 us: mix_rows(): comm_call(kernel, number, 2 * COMM_BYTES, out_shape=(jax.ShapeDtypeStruct...]
    reduce_scatter x3 -> x2, waiting for transfers between devices: 129 us -> 69.9 us  [the longest x1 69.9 us: body(): lax.psum_scatter(grad_gate_up_local, shards, scatter_dimension=0, tiled=T...]
    psum x1 -> x0, blocking collectives: 11.7 us -> none  [body(): gain_sums = lax.psum(gain_terms, 'tp')]
    unnamed x67 -> x71, local copies, waits for them, and re-layouts: 24.6 us -> 18.2 us
  transfers between devices with their start and end apart: 8 -> 6, of which waited for: 2 -> 1; matrix products, arithmetic and copies ran while one was open for 10% -> 9% of each run, Pallas kernels for 50% -> 46%
where the time goes in v2:
time: 675 us; the launch traced here: 666 us
  Pallas kernels  427 us (63%)
  matrix products  95.5 us (14%)
  waiting for transfers between devices  72.1 us (11%)
  local copies, waits for them, and re-layouts  31 us (5%)
  other arithmetic  25.2 us (4%)
  between operations  14.9 us (2%)
    pallas_call x2, Pallas kernels, mix_rows(): comm_call(kernel, number, 2 * COMM_BYTES, out_shape=(jax.ShapeDtypeStruct...  144 us
    reduce_scatter x1, waiting for transfers between devices, body(): lax.psum_scatter(grad_gate_up_local, shards, scatter_dimension=0, tiled=T...  69.9 us
    pallas_call x1, Pallas kernels, gather_blocks(): comm_call(kernel, number, COMM_BYTES, out_shape=(jax.ShapeDtypeStruct((pi...  57.1 us
    pallas_call x1, Pallas kernels, leave(): comm_call(kernel, number, COMM_BYTES, out_shape=(jax.ShapeDtypeStruct((pi...  53.3 us
    pallas_call x1, Pallas kernels, scatter_blocks(): comm_call(kernel, number, COMM_BYTES, out_shape=(jax.ShapeDtypeStruct((pi...  49.8 us
    pallas_call x1, Pallas kernels, enter(): comm_call(kernel, number, COMM_BYTES, out_shape=(jax.ShapeDtypeStruct((pi...  42.8 us
    pallas_call x1, Pallas kernels, attend_back(): pl.pallas_call(attend_back_kernel, out_shape=(jax.ShapeDtypeStruct((rows,...  41.3 us
    pallas_call x1, Pallas kernels, attend(): pl.pallas_call(attend_kernel, out_shape=(jax.ShapeDtypeStruct((rows, widt...  24.9 us
  transfers between devices with their start and end apart: 6, of which 1 were waited for; matrix products, arithmetic and copies ran while one was open for 9% of the time, Pallas kernels for 46%

profile of v2, /device:TPU:0, one launch (start us, length us, event | category | flops | bytes accessed | tf_op | source)
XLA Modules:
  0.0 666.2 jit_solution(14360490316495279701)
XLA Ops:
  22.0 42.8 %enter.1 = (bf16[2,4,64,2048]{3,2,1,0:T(8,128)(2,1)}, bf16[8,256,1536]{2,1,0:T(8,128)(2,1)}) custom-call(bf16[2,64,2048]{2,1,0:T(8,128)(2,1)S(1)} %fusion.3.x_ref, bf16[256,1536]{1,0:T(8,128)(2,1)S(1)} %multiply_convert_fusion.4.w_ref), custom_call_target="tpu_custom_call" | custom-call | bytes 134217728 | tf_op jit(solution)/shard_map/enter/pallas_call | solution.py:700
  71.8 8.7 %project.1 = (bf16[512,512]{1,0:T(8,128)(2,1)}, bf16[512,512]{1,0:T(8,128)(2,1)}, bf16[512,512]{1,0:T(8,128)(2,1)}) custom-call(bf16[512,2048]{1,0:T(8,128)(2,1)} %bitcast.87, bf16[2048,1536]{1,0:T(8,128)(2,1)} %bitcast.83, f32[512,128]{1,0:T(8,128)} %bitcast.77, f32[512,128]{1,0:T(8,128)} %bitcast.75), custom_call_target="tpu_custom_call" | custom-call | flops 3221225472 | bytes 8388608 | tf_op jit(solution)/shard_map/project/pallas_call | solution.py:239
  82.6 57.1 %gather_blocks.1 = (bf16[2,4,64,2048]{3,2,1,0:T(8,128)(2,1)}, bf16[4,512,512]{2,1,0:T(8,128)(2,1)}, bf16[4,512,512]{2,1,0:T(8,128)(2,1)}) custom-call(bf16[2,64,2048]{2,1,0:T(8,128)(2,1)S(1)} %bitcast.62, bf16[512,512]{1,0:T(8,128)(2,1)S(1)} %copy-done.7, bf16[512,512]{1,0:T(8,128)(2,1)S(1)} %copy-done.8), custom_call_target="tpu_custom_call" | custom-call | bytes 134217728 | tf_op jit(solution)/shard_map/gather_blocks/pallas_call | solution.py:731
  140.3 24.9 %attend.1 = (bf16[512,512]{1,0:T(8,128)(2,1)}, f32[4,4,256]{2,1,0:T(4,128)}) custom-call(s32[8]{0:T(128)} %bitcast.99, s32[2]{0:T(128)} %fusion.12.mine_ref, bf16[512,512]{1,0:T(8,128)(2,1)} %get-tuple-element.38.q_ref, bf16[8,256,512]{2,1,0:T(8,128)(2,1)} %bitcast.89, bf16[8,256,512]{2,1,0:T(8,128)(2,1)} %bitcast.91), custom_call_target="tpu_custom_call" | custom-call | flops 8589934592 | bytes 5242880 | tf_op jit(solution)/shard_map/attend/pallas_call | solution.py:82
  165.2 4.4 convolution_convert_fusion.6
  169.6 70.8 %mix_forward.1 = (f32[2,64,2048]{2,1,0:T(8,128)S(1)}, bf16[2,4,64,2048]{3,2,1,0:T(8,128)(2,1)}) custom-call(bf16[2,4,64,2048]{3,2,1,0:T(8,128)(2,1)} %bitcast.73, bf16[2,64,2048]{2,1,0:T(8,128)(2,1)S(1)} %bitcast.61), custom_call_target="tpu_custom_call" | custom-call | bytes 268435456 | tf_op jit(solution)/shard_map/mix_forward/pallas_call | solution.py:761
  241.4 15.1 %fusion.20 = f32[512,4096]{1,0:T(8,128)} fusion(bf16[512,2048]{1,0:T(8,128)(2,1)} %bitcast.97, bf16[2048,4096]{1,0:T(8,128)(2,1)} %all-gather.6.cloned.1.call-done), kind=kOutput, calls=%fused_computation.60 | convolution fusion | flops 8589934592 | bytes 27262976 | tf_op jit(solution)/shard_map/dot_general | solution.py:954
  256.5 12.2 %multiply_convert_fusion.1 = (bf16[512,2048]{1,0:T(8,128)(2,1)}, bf16[512,2048]{1,0:T(8,128)(2,1)}, bf16[512,2048]{1,0:T(8,128)(2,1)S(1)}) fusion(f32[512,4096]{1,0:T(8,128)} %fusion.20, bf16[512,2048]{1,0:T(8,128)(2,1)S(1)} %bitcast.93, bf16[2048,2048]{1,0:T(8,128)(2,1)} %all-gather.8.cloned.1.call-done), kind=kOutput, calls=%fused_computation.8 | convolution fusion | flops 4311744512 | bytes 25165824 | tf_op jit(solution)/shard_map/dot_general | solution.py:959
  270.1 6.9 %convolution_convert_fusion.2 = bf16[2048,2048]{1,0:T(8,128)(2,1)} fusion(bf16[512,2048]{1,0:T(8,128)(2,1)S(1)} %get-tuple-element.80, bf16[512,2048]{1,0:T(8,128)(2,1)S(1)} %bitcast.94), kind=kOutput, calls=%fused_computation.2 | convolution fusion | flops 4299161600 | bytes 12582912 | tf_op jit(solution)/shard_map/dot_general | solution.py:964
  277.0 15.2 %convolution_convert_fusion = bf16[2048,4096]{1,0:T(8,128)(2,1)} fusion(bf16[512,2048]{1,0:T(8,128)(2,1)} %bitcast.98, bf16[512,2048]{1,0:T(8,128)(2,1)} %get-tuple-element.79, bf16[512,2048]{1,0:T(8,128)(2,1)} %get-tuple-element.78), kind=kOutput, calls=%fused_computation | convolution fusion | flops 8606711808 | bytes 23068672 | tf_op jit(solution)/shard_map/dot_general | solution.py:968
  292.2 14.0 %convolution_convert_fusion.7 = bf16[512,2048]{1,0:T(8,128)(2,1)} fusion(bf16[2048,4096]{1,0:T(8,128)(2,1)} %all-gather.6.cloned.1.call-done, bf16[512,2048]{1,0:T(8,128)(2,1)} %get-tuple-element.79, bf16[512,2048]{1,0:T(8,128)(2,1)S(1)} %copy-done.30), kind=kOutput, calls=%fused_computation.16 | convolution fusion | flops 8599371776 | bytes 23068672 | tf_op jit(solution)/shard_map/dot_general | solution.py:972
  306.2 72.7 %mix_backward.1 = (f32[2,64,2048]{2,1,0:T(8,128)S(1)}, bf16[2,4,64,2048]{3,2,1,0:T(8,128)(2,1)}) custom-call(bf16[2,4,64,2048]{3,2,1,0:T(8,128)(2,1)} %bitcast.72, f32[2,64,2048]{2,1,0:T(8,128)} %copy-done.2, bf16[2,64,2048]{2,1,0:T(8,128)(2,1)S(1)} %bitcast.63), custom_call_target="tpu_custom_call" | custom-call | bytes 268435456 | tf_op jit(solution)/shard_map/mix_backward/pallas_call | solution.py:761
  379.9 4.2 convolution_convert_fusion.3
  386.3 3.8 convolution_convert_fusion.8.g_ref
  390.1 9.6 %convolution_convert_fusion.5 = bf16[512,2048]{1,0:T(8,128)(2,1)} fusion(bf16[512,2048]{1,0:T(8,128)(2,1)S(1)} %copy-done.29, bf16[2048,2048]{1,0:T(8,128)(2,1)} %all-gather.8.cloned.1.call-done), kind=kOutput, calls=%fused_computation.14 | convolution fusion | flops 4296015872 | bytes 12582912 | tf_op jit(solution)/shard_map/dot_general | solution.py:996
  399.7 41.3 %attend_back.1 = (bf16[512,512]{1,0:T(8,128)(2,1)}, bf16[8,256,512]{2,1,0:T(8,128)(2,1)}, bf16[8,256,512]{2,1,0:T(8,128)(2,1)}) custom-call(s32[8]{0:T(128)} %bitcast.100, s32[2]{0:T(128)} %fusion.12.mine_ref, bf16[512,512]{1,0:T(8,128)(2,1)} %get-tuple-element.38.q_ref, bf16[8,256,512]{2,1,0:T(8,128)(2,1)} %bitcast.90, bf16[8,256,512]{2,1,0:T(8,128)(2,1)} %bitcast.92, ...), custom_call_target="tpu_custom_call" | custom-call | flops 21474836480 | bytes 10485760 | tf_op jit(solution)/shard_map/attend_back/pallas_call | solution.py:178
  441.0 49.8 %scatter_blocks.1 = (f32[2,64,2048]{2,1,0:T(8,128)}, bf16[512,512]{1,0:T(8,128)(2,1)S(1)}, bf16[512,512]{1,0:T(8,128)(2,1)S(1)}) custom-call(bf16[2,4,64,2048]{3,2,1,0:T(8,128)(2,1)} %bitcast.69, bf16[4,512,512]{2,1,0:T(8,128)(2,1)} %bitcast.70, bf16[4,512,512]{2,1,0:T(8,128)(2,1)} %bitcast.71), custom_call_target="tpu_custom_call" | custom-call | bytes 134217728 | tf_op jit(solution)/shard_map/scatter_blocks/pallas_call | solution.py:796
  492.4 5.4 convolution_convert_fusion.1
  497.8 4.7 convolution_convert_fusion.4
  502.5 53.3 %leave.1 = (f32[2,64,2048]{2,1,0:T(8,128)S(1)}, f32[256,1536]{1,0:T(8,128)}) custom-call(bf16[2,4,64,2048]{3,2,1,0:T(8,128)(2,1)} %bitcast.74, bf16[8,256,1536]{2,1,0:T(8,128)(2,1)} %bitcast.67), custom_call_target="tpu_custom_call" | custom-call | bytes 134217728 | tf_op jit(solution)/shard_map/leave/pallas_call | solution.py:827
  570.7 69.9 %reduce-scatter.6.cloned.1.call-done = bf16[256,4096]{1,0:T(8,128)(2,1)} async-done(((bf16[2048,4096]{1,0:T(8,128)(2,1)}), bf16[256,4096]{1,0:T(8,128)(2,1)}) %reduce-scatter.6.cloned.1.call-update) | async-done | bytes 2097168 | tf_op jit(solution)/shard_map/reduce_scatter | solution.py:971
  640.6 5.6 convert_multiply_fusion
  646.2 6.6 reshape.160
  652.7 5.6 sum_small.1
  (116 shorter events, 46.8 us)
Async XLA Ops:
  7.2 4.5 copy-start.15
  7.2 158.0 %all-gather.4.cloned.1.call-start = ((), (), s32[]{:S(2)}) async-start(), calls=%async_computation.3 | async-start | bytes 2359296 | tf_op jit(solution)/shard_map/all_gather | solution.py:931
  7.9 10.3 %copy-start.21 = (f32[256]{0:T(256)}, f32[256]{0:T(256)S(1)}, u32[]{:S(2)}) copy-start(f32[256]{0:T(256)S(1)} %convert_element_type.95) | copy-start | bytes 3076
  8.6 9.8 %copy-start.19 = (f32[256]{0:T(256)}, f32[256]{0:T(256)S(1)}, u32[]{:S(2)}) copy-start(f32[256]{0:T(256)S(1)} %convert_element_type.89) | copy-start | bytes 3076
  22.0 44.3 %copy-start.26 = (s32[1,8]{1,0:T(1,128)S(1)}, s32[1,8]{1,0:T(1,128)}, u32[]{:S(2)}) copy-start(s32[1,8]{1,0:T(1,128)} %param.10) | copy-start | bytes 100
  64.8 176.6 %all-gather.6.cloned.1.call-start = ((), (), s32[]{:S(2)}) async-start(), calls=%async_computation.4 | async-start | bytes 18874368 | tf_op jit(solution)/shard_map/all_gather | solution.py:932
  65.6 190.9 %all-gather.8.cloned.1.call-start = ((), (), s32[]{:S(2)}) async-start(), calls=%async_computation.5 | async-start | bytes 9437184 | tf_op jit(solution)/shard_map/all_gather | solution.py:933
  66.3 499.9 %reduce-scatter.4.cloned.1.call-start = ((), (), s32[]{:S(2)}) async-start(), calls=%async_computation.6 | async-start | bytes 2359296 | tf_op jit(solution)/shard_map/reduce_scatter | solution.py:993
  70.2 10.3 %copy-start.12 = (f32[8,256,128]{2,1,0:T(8,128)}, f32[8,256,128]{2,1,0:T(8,128)S(1)}, u32[]{:S(2)}) copy-start(f32[8,256,128]{2,1,0:T(8,128)S(1)} %get-tuple-element.85.sin_ref) | copy-start | bytes 3145732
  70.2 10.3 %copy-start.13 = (f32[8,256,128]{2,1,0:T(8,128)}, f32[8,256,128]{2,1,0:T(8,128)S(1)}, u32[]{:S(2)}) copy-start(f32[8,256,128]{2,1,0:T(8,128)S(1)} %get-tuple-element.86.cos_ref) | copy-start | bytes 3145732
  71.8 8.7 %copy-start.4 = (bf16[1,2,64,2048]{3,2,1,0:T(8,128)(2,1)S(1)}, bf16[1,2,64,2048]{3,2,1,0:T(8,128)(2,1)}, u32[]{:S(2)}) copy-start(bf16[1,2,64,2048]{3,2,1,0:T(8,128)(2,1)} %param.17) | copy-start | bytes 1572868
  165.2 4.4 copy-start
  241.4 15.1 %copy-start.25 = (bf16[2,4,64,2048]{3,2,1,0:T(8,128)(2,1)S(1)}, bf16[2,4,64,2048]{3,2,1,0:T(8,128)(2,1)}, u32[]{:S(2)}) copy-start(bf16[2,4,64,2048]{3,2,1,0:T(8,128)(2,1)} %get-tuple-element.49) | copy-start | bytes 6291460
  277.0 15.2 %copy-start.30 = (bf16[512,2048]{1,0:T(8,128)(2,1)S(1)}, bf16[512,2048]{1,0:T(8,128)(2,1)}, u32[]{:S(2)}) copy-start(bf16[512,2048]{1,0:T(8,128)(2,1)} %get-tuple-element.78) | copy-start | bytes 6291460
  306.2 73.7 %copy-start.27 = (bf16[512,512]{1,0:T(8,128)(2,1)S(1)}, bf16[512,512]{1,0:T(8,128)(2,1)}, u32[]{:S(2)}) copy-start(bf16[512,512]{1,0:T(8,128)(2,1)} %get-tuple-element.43.o_ref) | copy-start | bytes 1572868
  384.1 183.9 %reduce-scatter.8.cloned.1.call-start = ((), (), s32[]{:S(2)}) async-start(), calls=%async_computation.8 | async-start | bytes 9437184 | tf_op jit(solution)/shard_map/reduce_scatter | solution.py:967
  384.7 255.8 %reduce-scatter.6.cloned.1.call-start = ((), (), s32[]{:S(2)}) async-start(), calls=%async_computation.7 | async-start | bytes 18874368 | tf_op jit(solution)/shard_map/reduce_scatter | solution.py:971
  441.0 49.8 %copy-start.16 = (bf16[512,512]{1,0:T(8,128)(2,1)S(1)}, bf16[512,512]{1,0:T(8,128)(2,1)}, u32[]{:S(2)}) copy-start(bf16[512,512]{1,0:T(8,128)(2,1)} %get-tuple-element.57) | copy-start | bytes 1572868
  441.0 56.8 %slice-start = ((s8[6291456]{0:T(1024)(128)(4,1)}), s8[2097152]{0:T(1024)(128)(4,1)S(1)}, s32[]{:S(2)}) async-start(s8[6291456]{0:T(1024)(128)(4,1)} %bitcast.84), calls=%async_computation.9 | async-start | bytes 4194304
  492.4 5.4 slice-start.1
  502.5 53.3 %copy-start.11 = (f32[256,1536]{1,0:T(8,128)S(1)}, f32[256,1536]{1,0:T(8,128)}, u32[]{:S(2)}) copy-start(f32[256,1536]{1,0:T(8,128)} %copy-done.10) | copy-start | bytes 4718596
  502.5 53.3 %copy-start.22 = (f32[256]{0:T(256)S(1)}, f32[256]{0:T(256)}, u32[]{:S(2)}) copy-start(f32[256]{0:T(256)} %copy-done.21) | copy-start | bytes 3076
  559.1 3.9 copy-start.3
  566.2 74.4 %copy-start.20 = (f32[256]{0:T(256)S(1)}, f32[256]{0:T(256)}, u32[]{:S(2)}) copy-start(f32[256]{0:T(256)} %copy-done.19) | copy-start | bytes 3076
  (15 other events, 28.7 us)
Sparse Core Ops, SparseCore 0:
  64.9 33.9 all-gather.3
  100.9 90.3 all-gather.5
  193.1 55.8 all-gather.7
  384.3 40.6 reduce-scatter.3
  428.3 87.0 reduce-scatter.7
  518.8 121.6 reduce-scatter.5
